TPU v7x, 32 devices: a whole 2x2x4 slice. The times are simulated.
32 devices in a mesh: fsdp: 32 (over z, y, x, core).
Axes of the slice: x: 2, y: 2, z: 4, core: 2. Of those that a mesh axis runs over, the one named last changes fastest.
Arguments:
- tok_ids: int32 [32, 256], P('fsdp')
- grad_out: bfloat16 [32, 256, 2048], P('fsdp')
- emb_table: bfloat16 [151936, 2048], P('fsdp')
- norm_gain: bfloat16 [2048], P('fsdp')
- w_query: bfloat16 [2048, 2048], P('fsdp')
- b_query: bfloat16 [2048], P('fsdp')
- w_key: bfloat16 [2048, 256], P('fsdp')
- b_key: bfloat16 [256], P('fsdp')
- w_value: bfloat16 [2048, 256], P('fsdp')
- b_value: bfloat16 [256], P('fsdp')
- w_out: bfloat16 [2048, 2048], P('fsdp')
Outputs:
- output 1: bfloat16 [32, 256, 2048], P('fsdp')
- output 2: bfloat16 [151936, 2048], P('fsdp')
- output 3: float32 [2048], P('fsdp')
- output 4: float32 [2048, 2048], P('fsdp')
- output 5: float32 [2048], P('fsdp')
- output 6: float32 [2048, 256], P('fsdp')
- output 7: float32 [256], P('fsdp')
- output 8: float32 [2048, 256], P('fsdp')
- output 9: float32 [256], P('fsdp')
- output 10: float32 [2048, 2048], P('fsdp')
All inputs are finite; a program needn't handle non-finite values.
Results may differ from a plain program's by a relative error of at most 0.0179842.
Values are sent between devices in bfloat16 or wider.
A program may use at most 1 GiB of HBM per device.

v0:
```python
import functools

import jax
import jax.numpy as jnp
from jax import lax
from jax.experimental import pallas as pl
from jax.experimental.pallas import tpu as pltpu
from jax.sharding import PartitionSpec as P

HEAD_DIM = 128
ROPE_THETA = 1.0e6
NORM_EPS = 1e-6
MASK_VALUE = -1e30
N_DEV = 32
HOT_CAP = 160
COLD_CAP = 16
QKV = 2560
WCOLS = 4608
MESH = pl.DeviceIdType.MESH


RELAYS = {2: (26, 18, 10, 6), 4: (28, 20, 12, 14), 8: (30, 22)}
N_RELAY = 4
RELAY_STEPS = (6, 9, 12, 15)


def far_blocks():
    out = []
    for k in range(N_RELAY):
        for via, ends in RELAYS.items():
            if k < len(ends):
                out.extend((ends[k] + core, via + core, k) for core in range(2))
    return out


def near_blocks():
    return [24, 25, 16, 17, 8, 9, 2, 3, 4, 5, 1]


def enter_all(me):
    barrier = pltpu.get_barrier_semaphore()

    def tell(off, carry):
        pl.semaphore_signal(barrier, inc=1, device_id=(lax.rem(me + off, N_DEV),), device_id_type=MESH)
        return carry

    lax.fori_loop(1, N_DEV, tell, 0)
    pl.semaphore_wait(barrier, N_DEV - 1)


def small_gather_kernel(src, dst, send_sem, recv_sem, own_sem):
    me = lax.axis_index("fsdp")
    enter_all(me)

    def copy(off):
        return pltpu.make_async_remote_copy(
            src_ref=src, dst_ref=dst.at[me], send_sem=send_sem.at[off], recv_sem=recv_sem.at[off],
            device_id=(lax.rem(me + off, N_DEV),), device_id_type=MESH)

    def start(off, carry):
        copy(off).start()
        return carry

    def finish(off, carry):
        copy(off).wait()
        return carry

    lax.fori_loop(1, N_DEV, start, 0)
    own = pltpu.make_async_copy(src, dst.at[me], own_sem)
    own.start()
    lax.fori_loop(1, N_DEV, finish, 0)
    own.wait()


def small_gather(block):
    return pl.pallas_call(
        small_gather_kernel,
        out_shape=jax.ShapeDtypeStruct((N_DEV,) + block.shape, block.dtype),
        in_specs=[pl.BlockSpec(memory_space=pltpu.VMEM)],
        out_specs=pl.BlockSpec(memory_space=pltpu.VMEM),
        scratch_shapes=[pltpu.SemaphoreType.DMA((N_DEV,)), pltpu.SemaphoreType.DMA((N_DEV,)), pltpu.SemaphoreType.DMA],
        compiler_params=pltpu.CompilerParams(collective_id=1, has_side_effects=True),
        name="small_gather",
    )(block)


def rows_at(ref, start, rows):
    return ref.at[pl.ds(pl.multiple_of(start, 16), rows)]


def on_relays(me, body):
    for via, ends in RELAYS.items():
        for core in range(2):
            @pl.when(me == via + core)
            def _(ends=ends, core=core):
                body([end + core for end in ends])


def lookup_kernel(send, hot_recv, cold_recv, relay, hs_sem, hr_sem, rr_sem, fs_sem, cs_sem, cr_sem, own_sem):
    me = lax.axis_index("fsdp")
    enter_all(me)

    def block(dev):
        return rows_at(send, dev * HOT_CAP, HOT_CAP)

    def near_copy(dev):
        return pltpu.make_async_remote_copy(
            src_ref=block(dev), dst_ref=hot_recv, send_sem=hs_sem.at[dev], recv_sem=hr_sem,
            device_id=(dev,), device_id_type=MESH)

    def far_copy(dev, via, k):
        return pltpu.make_async_remote_copy(
            src_ref=block(dev), dst_ref=relay.at[k], send_sem=hs_sem.at[dev], recv_sem=rr_sem.at[k],
            device_id=(via,), device_id_type=MESH)

    def cold_copy(off):
        other = lax.rem(me + off, N_DEV)
        return pltpu.make_async_remote_copy(
            src_ref=rows_at(send, other * HOT_CAP, COLD_CAP), dst_ref=rows_at(cold_recv, (me - 1) * COLD_CAP, COLD_CAP),
            send_sem=cs_sem.at[off], recv_sem=cr_sem.at[off], device_id=(other,), device_id_type=MESH)

    def cold_from(off):
        src = lax.rem(me - off + N_DEV, N_DEV)
        return src, pltpu.make_async_copy(
            rows_at(send, 0, COLD_CAP), rows_at(cold_recv, jnp.maximum(src - 1, 0) * COLD_CAP, COLD_CAP), cr_sem.at[off])

    own_hot = pltpu.make_async_copy(block(0), hot_recv, own_sem.at[0])
    own_cold = pltpu.make_async_copy(
        rows_at(send, me * HOT_CAP, COLD_CAP), rows_at(cold_recv, jnp.maximum(me - 1, 0) * COLD_CAP, COLD_CAP), own_sem.at[1])

    @pl.when(me == 0)
    def _():
        far, near = far_blocks(), near_blocks()
        for dev, via, k in far[:6]:
            far_copy(dev, via, k).start()
        for dev in near[:4]:
            near_copy(dev).start()
        for dev, via, k in far[6:]:
            far_copy(dev, via, k).start()
        for dev in near[4:]:
            near_copy(dev).start()
        own_hot.start()

    @pl.when(me != 0)
    def _():
        def start(off, carry):
            cold_copy(off).start()
            return carry

        lax.fori_loop(1, N_DEV, start, 0)
        own_cold.start()

    def pass_on(ends):
        def onward(k):
            return pltpu.make_async_remote_copy(
                src_ref=relay.at[k], dst_ref=hot_recv, send_sem=fs_sem.at[k], recv_sem=hr_sem,
                device_id=(ends[k],), device_id_type=MESH)

        for k in range(len(ends)):
            pltpu.make_async_copy(relay.at[k], relay.at[k], rr_sem.at[k]).wait()
            onward(k).start()
        for k in range(len(ends)):
            onward(k).wait_send()

    on_relays(me, pass_on)

    def arrived(off, carry):
        src, copy = cold_from(off)

        @pl.when(src != 0)
        def _():
            copy.wait()

        return carry

    lax.fori_loop(1, N_DEV, arrived, 0)

    @pl.when(me == 0)
    def _():
        own_hot.wait()
        for dev, via, k in far_blocks():
            far_copy(dev, via, k).wait_send()
        for dev in near_blocks():
            near_copy(dev).wait_send()

    @pl.when(me != 0)
    def _():
        pltpu.make_async_copy(hot_recv, hot_recv, hr_sem).wait()

        def sent(off, carry):
            cold_copy(off).wait_send()
            return carry

        lax.fori_loop(1, N_DEV, sent, 0)
        own_cold.wait()


def lookup_exchange(send):
    width = send.shape[1]
    dma = pltpu.SemaphoreType.DMA
    return pl.pallas_call(
        lookup_kernel,
        out_shape=(jax.ShapeDtypeStruct((HOT_CAP, width), jnp.bfloat16),
                   jax.ShapeDtypeStruct(((N_DEV - 1) * COLD_CAP, width), jnp.bfloat16)),
        in_specs=[pl.BlockSpec(memory_space=pl.ANY)],
        out_specs=(pl.BlockSpec(memory_space=pl.ANY),) * 2,
        scratch_shapes=[pltpu.VMEM((N_RELAY, HOT_CAP, width), jnp.bfloat16),
                        dma((N_DEV,)), dma, dma((N_RELAY,)), dma((N_RELAY,)), dma((N_DEV,)), dma((N_DEV,)), dma((2,))],
        compiler_params=pltpu.CompilerParams(collective_id=2, has_side_effects=True),
        cost_estimate=pl.CostEstimate(flops=60_000_000_000, bytes_accessed=30_000_000, transcendentals=0),
        name="lookup_exchange",
    )(send)


def return_kernel(hot_send, cold_send, vec_send, own, oth, recv, vec_recv, out, relay,
                  held, got0, send1, keep1, got1, send2, keep2, got2, send3, keep3, got3,
                  held_sem, s0_sem, r0_sem, s1_sem, r1_sem, s2_sem, r2_sem, s3_sem, r3_sem, hs_sem, hr_sem, rr_sem, fs_sem, cs_sem, cr_sem, vs_sem, vr_sem, own_sem):
    me = lax.axis_index("fsdp")
    enter_all(me)

    def block(dev):
        return rows_at(recv, dev * HOT_CAP, HOT_CAP)

    def near_copy(dev):
        return pltpu.make_async_remote_copy(
            src_ref=hot_send, dst_ref=block(dev), send_sem=hs_sem, recv_sem=hr_sem.at[dev],
            device_id=(0,), device_id_type=MESH)

    def far_copy(via, k):
        return pltpu.make_async_remote_copy(
            src_ref=hot_send, dst_ref=relay.at[k], send_sem=hs_sem, recv_sem=rr_sem.at[k],
            device_id=(via,), device_id_type=MESH)

    def vec_copy(off):
        other = lax.rem(me + off, N_DEV)
        return pltpu.make_async_remote_copy(
            src_ref=vec_send.at[other], dst_ref=vec_recv.at[me], send_sem=vs_sem.at[off], recv_sem=vr_sem.at[off],
            device_id=(other,), device_id_type=MESH)

    def cold_copy(off):
        other = lax.rem(me + off, N_DEV)
        return other, pltpu.make_async_remote_copy(
            src_ref=rows_at(cold_send, jnp.maximum(other - 1, 0) * COLD_CAP, COLD_CAP),
            dst_ref=rows_at(recv, me * HOT_CAP, COLD_CAP),
            send_sem=cs_sem.at[off], recv_sem=cr_sem.at[off], device_id=(other,), device_id_type=MESH)

    def cold_from(off):
        src = lax.rem(me - off + N_DEV, N_DEV)
        return pltpu.make_async_copy(
            rows_at(cold_send, 0, COLD_CAP), rows_at(recv, src * HOT_CAP, COLD_CAP), cr_sem.at[off])

    own_hot = pltpu.make_async_copy(hot_send, block(0), own_sem.at[0])
    own_cold = pltpu.make_async_copy(
        rows_at(cold_send, jnp.maximum(me - 1, 0) * COLD_CAP, COLD_CAP), rows_at(recv, me * HOT_CAP, COLD_CAP), own_sem.at[1])
    own_vec = pltpu.make_async_copy(vec_send.at[me], vec_recv.at[me], own_sem.at[2])

    for dev in near_blocks():
        @pl.when(me == dev)
        def _(dev=dev):
            near_copy(dev).start()

    for dev, via, k in far_blocks():
        @pl.when(me == dev)
        def _(via=via, k=k):
            far_copy(via, k).start()

    def start(off, carry):
        other, copy = cold_copy(off)

        @pl.when(other != 0)
        def _():
            copy.start()

        vec_copy(off).start()
        return carry

    lax.fori_loop(1, N_DEV, start, 0)
    own_vec.start()

    @pl.when(me == 0)
    def _():
        own_hot.start()

    @pl.when(me != 0)
    def _():
        own_cold.start()

    groups, half, width = own.shape
    core, x, y, z = lax.rem(me, 2), lax.rem(me // 2, 2), lax.rem(me // 4, 2), me // 8
    first = jnp.where(core == 0, x, y)
    second = jnp.where(core == 0, y, x)
    span = jnp.where(core == 0, 2, 4)
    near1 = me + span * (1 - 2 * first)
    near2 = me + (6 - span) * (1 - 2 * second)
    f32, bf16 = jnp.float32, jnp.bfloat16

    def part(size, index):
        return pl.ds(pl.multiple_of(index * size, size), size)

    def to(src, dst, send_sem, recv_sem, dev):
        return pltpu.make_async_remote_copy(src_ref=src, dst_ref=dst, send_sem=send_sem, recv_sem=recv_sem,
                                            device_id=(dev,), device_id_type=MESH)

    def copy0(g):
        return to(oth.at[g], got0.at[g], s0_sem, r0_sem.at[g], me + 1 - 2 * core)

    def load(g):
        return pltpu.make_async_copy(own.at[g], held.at[lax.rem(g, 2)], held_sem.at[lax.rem(g, 2)])

    def copy1(g):
        return to(send1.at[g], got1.at[g], s1_sem, r1_sem.at[g], near1)

    def copy2(g):
        return to(send2.at[g], got2.at[g], s2_sem, r2_sem.at[g], near2)

    def copy3(g, dz):
        peer = lax.rem(z + dz, 4)
        return to(send3.at[g, dz - 1], got3.at[g, dz - 1], s3_sem, r3_sem.at[g, dz - 1], me + 8 * (peer - z))

    load(0).start()
    load(1).start()

    def start0(g, carry):
        copy0(g).start()
        return carry

    lax.fori_loop(0, groups, start0, 0)

    def stage(lag, step, body):
        g = step - lag

        @pl.when((g >= 0) & (g < groups))
        def _():
            body(g, lax.rem(g + 3, 3))

    def across_core(g, slot):
        copy0(g).wait_recv()
        load(g).wait()
        here = held.at[lax.rem(g, 2)]
        for sent in range(2):
            rows = part(half // 2, 1 - first if sent else first)
            total = here[rows, :] + got0[g, rows, :].astype(f32)
            if sent:
                send1[g] = total.astype(bf16)
            else:
                keep1[slot] = total
        copy1(g).start()

        @pl.when(g + 2 < groups)
        def _():
            load(g + 2).start()

    def across_first(g, slot):
        copy1(g).wait_recv()
        for sent in range(2):
            rows = part(half // 4, 1 - second if sent else second)
            total = keep1[slot, rows, :] + got1[g, rows, :].astype(f32)
            if sent:
                send2[g] = total.astype(bf16)
            else:
                keep2[slot] = total
        copy2(g).start()

    def across_second(g, slot):
        copy2(g).wait_recv()
        for dz in range(1, 4):
            rows = part(half // 16, lax.rem(z + dz, 4))
            send3[g, dz - 1] = (keep2[slot, rows, :] + got2[g, rows, :].astype(f32)).astype(bf16)
        rows = part(half // 16, z)
        keep3[slot] = keep2[slot, rows, :] + got2[g, rows, :].astype(f32)
        for dz in range(1, 4):
            copy3(g, dz).start()

    def across_z(g, slot):
        total = keep3[slot]
        for dz in range(1, 4):
            copy3(g, dz).wait_recv()
            total = total + got3[g, dz - 1].astype(f32)
        out[:, pl.ds(pl.multiple_of(g * width, width), width)] = total

    def onward(ends, k):
        return to(relay.at[k], block(ends[k]), fs_sem.at[k], hr_sem.at[ends[k]], 0)

    def run(step, carry):
        stage(0, step, across_core)
        stage(2, step, across_first)
        stage(4, step, across_second)
        stage(6, step, across_z)

        def pass_on(ends):
            for k in reversed(range(len(ends))):
                @pl.when(step == RELAY_STEPS[N_RELAY - 1 - k])
                def _(k=k):
                    pltpu.make_async_copy(relay.at[k], relay.at[k], rr_sem.at[k]).wait()
                    onward(ends, k).start()

        on_relays(me, pass_on)
        return carry

    lax.fori_loop(0, groups + 6, run, 0)

    def passed(ends):
        for k in range(len(ends)):
            onward(ends, k).wait_send()

    on_relays(me, passed)

    for buf, sem in ((got0, s0_sem), (send1, s1_sem), (send2, s2_sem), (send3, s3_sem)):
        pltpu.make_async_copy(buf, buf, sem).wait()

    def finish(off, carry):
        other, copy = cold_copy(off)

        @pl.when(other != 0)
        def _():
            copy.wait_send()

        vec_copy(off).wait()
        return carry

    lax.fori_loop(1, N_DEV, finish, 0)
    own_vec.wait()

    @pl.when(me != 0)
    def _():
        def arrived(off, carry):
            cold_from(off).wait()
            return carry

        lax.fori_loop(1, N_DEV, arrived, 0)
        own_cold.wait()
        far_copy(2, 0).wait_send()

    @pl.when(me == 0)
    def _():
        own_hot.wait()

        def arrived(dev, carry):
            pltpu.make_async_copy(block(dev), block(dev), hr_sem.at[dev]).wait()
            return carry

        lax.fori_loop(1, N_DEV, arrived, 0)


def return_exchange(hot_send, cold_send, vec_send, own, oth):
    width = hot_send.shape[1]
    groups, half, cols = own.shape
    dma = pltpu.SemaphoreType.DMA
    f32, bf16 = jnp.float32, jnp.bfloat16
    anywhere = pl.BlockSpec(memory_space=pl.ANY)
    return pl.pallas_call(
        return_kernel,
        out_shape=(jax.ShapeDtypeStruct((N_DEV * HOT_CAP, width), bf16),
                   jax.ShapeDtypeStruct(vec_send.shape, f32),
                   jax.ShapeDtypeStruct((half // 16, groups * cols), f32)),
        in_specs=[anywhere] * 5,
        out_specs=(anywhere, anywhere, pl.BlockSpec(memory_space=pltpu.VMEM)),
        scratch_shapes=[pltpu.VMEM((N_RELAY, HOT_CAP, width), bf16),
                        pltpu.VMEM((2, half, cols), f32), pltpu.VMEM((groups, half, cols), bf16),
                        pltpu.VMEM((groups, half // 2, cols), bf16), pltpu.VMEM((3, half // 2, cols), f32),
                        pltpu.VMEM((groups, half // 2, cols), bf16),
                        pltpu.VMEM((groups, half // 4, cols), bf16), pltpu.VMEM((3, half // 4, cols), f32),
                        pltpu.VMEM((groups, half // 4, cols), bf16),
                        pltpu.VMEM((groups, 3, half // 16, cols), bf16), pltpu.VMEM((3, half // 16, cols), f32),
                        pltpu.VMEM((groups, 3, half // 16, cols), bf16),
                        dma((2,)), dma, dma((groups,)), dma, dma((groups,)), dma, dma((groups,)), dma, dma((groups, 3)),
                        dma, dma((N_DEV,)), dma((N_RELAY,)), dma((N_RELAY,)), dma((N_DEV,)), dma((N_DEV,)),
                        dma((N_DEV,)), dma((N_DEV,)), dma((3,))],
        compiler_params=pltpu.CompilerParams(collective_id=3, has_side_effects=True, vmem_limit_bytes=56 * 1024 * 1024),
        cost_estimate=pl.CostEstimate(flops=60_000_000_000, bytes_accessed=60_000_000, transcendentals=0),
        name="return_exchange",
    )(hot_send, cold_send, vec_send, own, oth)


GROUP = 256
CHUNK = 64


def weight_grad_kernel(hidden_ref, attn_ref, g_ref, own_ref, oth_ref):
    step = pl.program_id(0)
    core = lax.rem(lax.axis_index("fsdp"), 2)
    dims = (((0,), (0,)), ((), ()))

    def place(lhs_ref):
        res = lax.dot_general(lhs_ref[...], g_ref[...], dims, preferred_element_type=jnp.float32)
        for mine in range(2):
            @pl.when(core == mine)
            def _(mine=mine):
                for dev in range(N_DEV):
                    z, y, x, c = dev // 8, dev // 4 % 2, dev // 2 % 2, dev % 2
                    spot = ((x * 2 + y) if c == 0 else (y * 2 + x)) * 4 + z
                    chunk = res[dev * CHUNK:(dev + 1) * CHUNK]
                    if c == mine:
                        own_ref[0, spot * CHUNK:(spot + 1) * CHUNK, :] = chunk
                    else:
                        oth_ref[0, spot * CHUNK:(spot + 1) * CHUNK, :] = chunk.astype(jnp.bfloat16)

    @pl.when(step < QKV // GROUP)
    def _():
        place(hidden_ref)

    @pl.when(step >= QKV // GROUP)
    def _():
        place(attn_ref)


def weight_grads(hidden, attn_b, grads):
    tokens, width = hidden.shape
    groups, half = WCOLS // GROUP, width // 2
    return pl.pallas_call(
        weight_grad_kernel,
        grid=(groups,),
        out_shape=(jax.ShapeDtypeStruct((groups, half, GROUP), jnp.float32),
                   jax.ShapeDtypeStruct((groups, half, GROUP), jnp.bfloat16)),
        in_specs=[pl.BlockSpec((tokens, width), lambda j: (0, 0)),
                  pl.BlockSpec((tokens, width), lambda j: (0, 0)),
                  pl.BlockSpec((tokens, GROUP), lambda j: (0, j))],
        out_specs=(pl.BlockSpec((1, half, GROUP), lambda j: (j, 0, 0)),) * 2,
        compiler_params=pltpu.CompilerParams(vmem_limit_bytes=40 * 1024 * 1024),
        cost_estimate=pl.CostEstimate(flops=2 * tokens * width * WCOLS, bytes_accessed=width * WCOLS * 3, transcendentals=0),
        name="weight_grads",
    )(hidden, attn_b, grads)


SLOTS = 16
TILE = 128


def table_sum_kernel(low_ref, high_ref, dx_ref, row_ref, out_ref, total):
    step = pl.program_id(0)
    n_groups = HOT_CAP // SLOTS
    tiles = total.shape[0] // TILE

    def tile(index):
        return pl.ds(pl.multiple_of(index * TILE, TILE), TILE)

    @pl.when(step == 0)
    def _():
        def clear(index, carry):
            total[tile(index), :] = jnp.zeros((TILE, total.shape[1]), jnp.float32)
            return carry

        lax.fori_loop(0, tiles, clear, 0)

    @pl.when(step < n_groups)
    def _():
        dx = dx_ref[...].reshape(-1, dx_ref.shape[2])
        rows = row_ref[0]

        def add(index, carry):
            place = index * TILE + lax.broadcasted_iota(jnp.int32, (TILE, rows.shape[1]), 0)
            pick = jnp.where(place == rows, 1.0, 0.0).astype(jnp.bfloat16)
            total[tile(index), :] += jnp.dot(pick, dx, preferred_element_type=jnp.float32)
            return carry

        at = jnp.minimum(step, n_groups - 1)
        lax.fori_loop(low_ref[at], high_ref[at], add, 0)

    @pl.when(step >= n_groups)
    def _():
        out_ref[...] = total[tile(jnp.maximum(step - n_groups, 0)), :].astype(jnp.bfloat16)


def table_sum(dx_recv, rows, rows_dev):
    width = dx_recv.shape[1]
    n_groups = HOT_CAP // SLOTS
    tiles = (rows_dev + TILE - 1) // TILE
    by_group = rows.reshape(N_DEV, n_groups, SLOTS).transpose(1, 0, 2).reshape(n_groups, 1, N_DEV * SLOTS)
    valid = by_group >= 0
    low = jnp.min(jnp.where(valid, by_group, rows_dev), axis=(1, 2)) // TILE
    high = jnp.max(jnp.where(valid, by_group + TILE, 0), axis=(1, 2)) // TILE
    return pl.pallas_call(
        table_sum_kernel,
        grid_spec=pltpu.PrefetchScalarGridSpec(
            num_scalar_prefetch=2,
            grid=(n_groups + tiles,),
            in_specs=[pl.BlockSpec((N_DEV, SLOTS, width), lambda s, lo, hi: (0, jnp.minimum(s, n_groups - 1), 0)),
                      pl.BlockSpec((1, 1, N_DEV * SLOTS), lambda s, lo, hi: (jnp.minimum(s, n_groups - 1), 0, 0))],
            out_specs=pl.BlockSpec((TILE, width), lambda s, lo, hi: (jnp.maximum(s - n_groups, 0), 0)),
            scratch_shapes=[pltpu.VMEM((tiles * TILE, width), jnp.float32)]),
        out_shape=jax.ShapeDtypeStruct((rows_dev, width), jnp.bfloat16),
        compiler_params=pltpu.CompilerParams(vmem_limit_bytes=56 * 1024 * 1024),
        cost_estimate=pl.CostEstimate(flops=30_000_000_000, bytes_accessed=45_000_000, transcendentals=0),
        name="table_sum",
    )(low, high, dx_recv.reshape(N_DEV, HOT_CAP, width), by_group)


Q_GROUP = 8
KV_HEADS = 2


def turn(vector):
    return pltpu.roll(vector, HEAD_DIM // 2, 1)


def attention_kernel(q_ref, k_ref, v_ref, d_attn_ref, cos_ref, sin_ref,
                     attn_ref, dq_ref, dk_ref, dv_ref, gq_ref, gk_ref, gv_ref, k_rot, v_val, dk_sum, dv_sum):
    member = lax.rem(pl.program_id(0), Q_GROUP)
    scale = HEAD_DIM ** -0.5
    cos_t, sin_t = cos_ref[...], sin_ref[...]
    rows_t = (((1,), (1,)), ((), ()))
    cols_t = (((0,), (0,)), ((), ()))
    f32 = jnp.float32

    @pl.when(member == 0)
    def _():
        k_lin = k_ref[...]
        k_rot[...] = (k_lin * cos_t + turn(k_lin) * sin_t).astype(jnp.bfloat16)
        v_val[...] = v_ref[...].astype(jnp.bfloat16)
        dk_sum[...] = jnp.zeros_like(dk_sum)
        dv_sum[...] = jnp.zeros_like(dv_sum)

    q_lin = q_ref[...]
    q_rot = (q_lin * cos_t + turn(q_lin) * sin_t).astype(jnp.bfloat16)
    scores = lax.dot_general(q_rot, k_rot[...], rows_t, preferred_element_type=f32) * scale
    seq = scores.shape[0]
    causal = lax.broadcasted_iota(jnp.int32, (seq, seq), 0) >= lax.broadcasted_iota(jnp.int32, (seq, seq), 1)
    scores = jnp.where(causal, scores, MASK_VALUE)
    weight = jnp.exp(scores - jnp.max(scores, axis=1, keepdims=True))
    prob_f = weight / jnp.sum(weight, axis=1, keepdims=True)
    prob_b = prob_f.astype(jnp.bfloat16)
    attn_ref[...] = jnp.dot(prob_b, v_val[...], preferred_element_type=f32).astype(jnp.bfloat16)

    d_attn = d_attn_ref[...]
    d_probs = lax.dot_general(d_attn, v_val[...], rows_t, preferred_element_type=f32)
    dv_sum[...] += lax.dot_general(prob_b, d_attn, cols_t, preferred_element_type=f32)
    d_scores = prob_f * (d_probs - jnp.sum(d_probs * prob_f, axis=1, keepdims=True))
    d_scores = (d_scores * scale).astype(jnp.bfloat16)
    d_qrot = jnp.dot(d_scores, k_rot[...], preferred_element_type=f32)
    dk_sum[...] += lax.dot_general(d_scores, q_rot, cols_t, preferred_element_type=f32)
    d_query = d_qrot * cos_t - turn(d_qrot) * sin_t
    dq_ref[...] = d_query.astype(jnp.bfloat16)
    gq_ref[...] = jnp.sum(d_query, axis=0, keepdims=True)

    @pl.when(member == Q_GROUP - 1)
    def _():
        d_krot = dk_sum[...]
        d_key = d_krot * cos_t - turn(d_krot) * sin_t
        d_value = dv_sum[...]
        dk_ref[...] = d_key.astype(jnp.bfloat16)
        dv_ref[...] = d_value.astype(jnp.bfloat16)
        gk_ref[...] = jnp.sum(d_key, axis=0, keepdims=True)
        gv_ref[...] = jnp.sum(d_value, axis=0, keepdims=True)


def attention(lin, d_attn, cos_t, sin_t):
    seq = lin.shape[0]
    heads = KV_HEADS * Q_GROUP

    def cols(index):
        return pl.BlockSpec((seq, HEAD_DIM), lambda h: (0, index(h)))

    def line(index):
        return pl.BlockSpec((1, HEAD_DIM), lambda h: (0, index(h)))

    def shape(rows, width, dtype):
        return jax.ShapeDtypeStruct((rows, width), dtype)

    q_width, kv_width = heads * HEAD_DIM, KV_HEADS * HEAD_DIM
    own = lambda h: h
    group = lambda h: h // Q_GROUP
    first = lambda h: 0
    return pl.pallas_call(
        attention_kernel,
        grid=(heads,),
        in_specs=[cols(own), cols(lambda h: heads + h // Q_GROUP), cols(lambda h: heads + KV_HEADS + h // Q_GROUP),
                  cols(own), cols(first), cols(first)],
        out_specs=(cols(own), cols(own), cols(group), cols(group), line(own), line(group), line(group)),
        out_shape=(shape(seq, q_width, jnp.bfloat16), shape(seq, q_width, jnp.bfloat16),
                   shape(seq, kv_width, jnp.bfloat16), shape(seq, kv_width, jnp.bfloat16),
                   shape(1, q_width, jnp.float32), shape(1, kv_width, jnp.float32), shape(1, kv_width, jnp.float32)),
        scratch_shapes=[pltpu.VMEM((seq, HEAD_DIM), jnp.bfloat16), pltpu.VMEM((seq, HEAD_DIM), jnp.bfloat16),
                        pltpu.VMEM((seq, HEAD_DIM), jnp.float32), pltpu.VMEM((seq, HEAD_DIM), jnp.float32)],
        cost_estimate=pl.CostEstimate(flops=14 * seq * seq * q_width, bytes_accessed=10_000_000, transcendentals=heads * seq * seq),
        name="attention",
    )(lin, lin, lin, d_attn, cos_t, sin_t)


def block_fwd_bwd(x_rows, grad_out, gain_vec, w_all, b_qkv):
    seq_len = x_rows.shape[0]
    w_qkv = w_all[:, :QKV]
    w_out = w_all[:, QKV:]
    half_dim = HEAD_DIM // 2
    inv_freq = jnp.power(ROPE_THETA, -(jnp.arange(half_dim, dtype=jnp.float32) * 2.0 / HEAD_DIM))
    angles = jnp.arange(seq_len, dtype=jnp.float32)[:, None] * inv_freq[None, :]
    cos_h, sin_h = jnp.cos(angles), jnp.sin(angles)
    cos_t = jnp.concatenate([cos_h, cos_h], axis=1)
    sin_t = jnp.concatenate([-sin_h, sin_h], axis=1)
    x_full = x_rows.astype(jnp.float32)
    inv_rms = lax.rsqrt(jnp.mean(x_full * x_full, axis=-1, keepdims=True) + NORM_EPS)
    x_norm = x_full * inv_rms
    gain_f = gain_vec.astype(jnp.float32)
    hidden = (x_norm * gain_f).astype(jnp.bfloat16)
    lin = jnp.dot(hidden, w_qkv, preferred_element_type=jnp.float32) + b_qkv.astype(jnp.float32)
    d_attn = jnp.einsum("lo,io->li", grad_out, w_out, preferred_element_type=jnp.float32).astype(jnp.bfloat16)
    attn_b, dq_b, dk_b, dv_b, grad_bq, grad_bk, grad_bv = attention(lin, d_attn, cos_t, sin_t)
    proj_out = jnp.dot(attn_b, w_out, preferred_element_type=jnp.float32)
    block_out = (x_full + proj_out).astype(jnp.bfloat16)
    d_lin_b = jnp.concatenate([dq_b, dk_b, dv_b], axis=1)
    grad_w = weight_grads(hidden, attn_b, jnp.concatenate([d_lin_b, grad_out], axis=1))
    d_hidden = jnp.einsum("lo,io->li", d_lin_b, w_qkv, preferred_element_type=jnp.float32)
    grad_gain = jnp.sum(d_hidden * x_norm, axis=0)
    d_norm = d_hidden * gain_f
    d_x = grad_out.astype(jnp.float32) + inv_rms * (d_norm - x_norm * jnp.mean(d_norm * x_norm, axis=-1, keepdims=True))
    grad_b = jnp.concatenate([grad_bq[0], grad_bk[0], grad_bv[0]])
    return block_out, d_x, grad_w, grad_gain, grad_b


def solution(mesh):
    row_spec = P("fsdp", None)
    vec_spec = P("fsdp")
    act_spec = P("fsdp", None, None)
    weight_specs = (vec_spec, row_spec, vec_spec, row_spec, vec_spec, row_spec, vec_spec, row_spec)
    in_specs = (row_spec, act_spec, row_spec) + weight_specs
    out_specs = (act_spec, row_spec) + weight_specs

    def device_step(tok_ids, grad_out, table_part, gain_part, wq_part, bq_part, wk_part, bk_part, wv_part, bv_part, wo_part):
        rows_dev, model_width = table_part.shape
        seq_len = tok_ids.shape[1]
        me = lax.axis_index("fsdp")
        first_row = me * rows_dev
        w_all = lax.all_gather(jnp.concatenate([wq_part, wk_part, wv_part, wo_part], axis=1), "fsdp", axis=0, tiled=True)

        vec_part = jnp.concatenate([gain_part, bq_part, bk_part, bv_part]).astype(jnp.float32)
        block = jnp.concatenate([tok_ids.reshape(-1).astype(jnp.float32), jnp.pad(vec_part, (0, 1024 - 256 - 144))])
        gathered = small_gather(block.reshape(8, 128)).reshape(N_DEV, 1024)
        all_ids = gathered[:, :seq_len].astype(jnp.int32)
        vecs = gathered[:, seq_len:seq_len + 144].astype(jnp.bfloat16)
        gain_full = vecs[:, :64].reshape(-1)
        b_qkv = jnp.concatenate([vecs[:, 64:128].reshape(-1), vecs[:, 128:136].reshape(-1), vecs[:, 136:144].reshape(-1)])

        owner = all_ids // rows_dev
        key = all_ids * seq_len + jnp.arange(seq_len)
        counts = jnp.sum((owner[:, :, None] == jnp.arange(N_DEV)).astype(jnp.int32), axis=1)
        overflow = (jnp.max(counts[:, 0]) > HOT_CAP) | (jnp.max(counts[:, 1:]) > COLD_CAP)

        mask = owner == me
        rank = jnp.sum((mask[:, None, :] & (key[:, None, :] < key[:, :, None])).astype(jnp.int32), axis=2)
        hit = mask[:, None, :] & (rank[:, None, :] == jnp.arange(HOT_CAP)[None, :, None])
        rows = jnp.sum(jnp.where(hit, (all_ids - first_row)[:, None, :] + 1, 0), axis=2).reshape(-1) - 1
        hot_recv, cold_recv = lookup_exchange(jnp.take(table_part, jnp.maximum(rows, 0), axis=0, mode="clip"))

        my_ids = tok_ids.reshape(-1)
        my_owner = my_ids // rows_dev
        my_key = my_ids * seq_len + jnp.arange(seq_len)
        same = (my_owner[:, None] == my_owner[None, :]) & (my_key[None, :] < my_key[:, None])
        my_rank = jnp.sum(same.astype(jnp.int32), axis=1)
        hot_slot = jnp.where(my_owner == 0, my_rank, -1)
        cold_slot = jnp.where(my_owner > 0, (my_owner - 1) * COLD_CAP + my_rank, -1)
        hot_pick = (hot_slot[:, None] == jnp.arange(HOT_CAP)[None, :]).astype(jnp.bfloat16)
        cold_pick = (cold_slot[:, None] == jnp.arange((N_DEV - 1) * COLD_CAP)[None, :]).astype(jnp.bfloat16)

        def rows_fast():
            picked = jnp.dot(hot_pick, hot_recv, preferred_element_type=jnp.float32)
            picked = picked + jnp.dot(cold_pick, cold_recv, preferred_element_type=jnp.float32)
            return picked.astype(jnp.bfloat16)

        ring = [(i, (i + 1) % N_DEV) for i in range(N_DEV)]

        def owned_rows(step):
            local_idx = jnp.take(all_ids, lax.rem(me - step + N_DEV, N_DEV), axis=0) - first_row
            return local_idx, (local_idx >= 0) & (local_idx < rows_dev)

        def rows_ring():
            def body(step, acc):
                local_idx, is_owned = owned_rows(step)
                looked = jnp.take(table_part, jnp.where(is_owned, local_idx, 0), axis=0, mode="clip")
                acc = jnp.where(is_owned[:, None], looked, acc)
                return lax.ppermute(acc, "fsdp", ring)

            return lax.fori_loop(0, N_DEV, body, jnp.zeros((seq_len, model_width), jnp.bfloat16))

        x_rows = lax.cond(overflow, rows_ring, rows_fast)
        g_rows = grad_out.reshape(seq_len, model_width)
        block_out, d_x, grad_w, grad_gain, grad_b = block_fwd_bwd(x_rows, g_rows, gain_full, w_all, b_qkv)
        dx_b = d_x.astype(jnp.bfloat16)
        tdims = (((0,), (0,)), ((), ()))
        hot_back = lax.dot_general(hot_pick, dx_b, tdims, preferred_element_type=jnp.float32).astype(jnp.bfloat16)
        cold_back = lax.dot_general(cold_pick, dx_b, tdims, preferred_element_type=jnp.float32).astype(jnp.bfloat16)
        vec_grad = jnp.concatenate(
            [grad_gain.reshape(N_DEV, 64), grad_b[:2048].reshape(N_DEV, 64), grad_b[2048:2304].reshape(N_DEV, 8),
             grad_b[2304:].reshape(N_DEV, 8), jnp.zeros((N_DEV, 1024 - 144), jnp.float32)], axis=1)
        dx_recv, vec_sum, w_red = return_exchange(hot_back, cold_back, vec_grad.reshape(N_DEV, 8, 128), *grad_w)

        def table_fast():
            return table_sum(dx_recv, rows, rows_dev)

        def table_ring():
            def body(step, carry):
                total, moving = carry
                local_idx, is_owned = owned_rows(step)
                seg_idx = jnp.where(is_owned, local_idx, rows_dev)
                total = total.at[seg_idx].add(moving.astype(jnp.float32), mode="drop")
                return total, lax.ppermute(moving, "fsdp", ring)

            start = (jnp.zeros((rows_dev, model_width), jnp.float32), dx_b)
            return lax.fori_loop(0, N_DEV, body, start)[0].astype(jnp.bfloat16)

        grad_table = lax.cond(overflow, table_ring, table_fast)
        v_red = jnp.sum(vec_sum.reshape(N_DEV, 1024), axis=0)
        return (block_out[None], grad_table, v_red[:64], w_red[:, :2048], v_red[64:128], w_red[:, 2048:2304],
                v_red[128:136], w_red[:, 2304:2560], v_red[136:144], w_red[:, 2560:])

    return jax.shard_map(device_step, mesh=mesh, in_specs=in_specs, out_specs=out_specs, check_vma=False)
```

profile of v0, /device:TPU:0, one launch (start us, length us, event | category | flops | bytes accessed | tf_op | source)
XLA Modules:
  0.0 613.1 jit_solution(2825897229142641818)
XLA Ops:
  7.2 1.9 pad_maximum_fusion.1
  11.3 12.6 %small_gather.1 = f32[32,8,128]{2,1,0:T(8,128)} custom-call(f32[8,128]{1,0:T(8,128)} %maximum_bitcast_fusion.src), custom_call_target="tpu_custom_call" | custom-call | tf_op jit(solution)/shard_map/small_gather/pallas_call | solution.py:76
  30.6 2.6 convert_reduce_fusion
  35.2 47.9 %gather_fusion.1 = bf16[5120,2048]{1,0:T(8,128)(2,1)} fusion(bf16[4748,2048]{1,0:T(8,128)(2,1)} %param.23, s32[5120]{0:T(1024)S(1)} %broadcast_clamp_fusion), kind=kCustom, calls=%fused_computation.1 | custom fusion | bytes 41963520 | tf_op jit(solution)/shard_map/jit(_take)/gather | solution.py:741
  83.6 134.7 %lookup_exchange.1 = (bf16[160,2048]{1,0:T(8,128)(2,1)S(1)}, bf16[496,2048]{1,0:T(8,128)(2,1)}) custom-call(bf16[5120,2048]{1,0:T(8,128)(2,1)} %gather_fusion.1), custom_call_target="tpu_custom_call" | custom-call | flops 60000002048 | bytes 30000000 | tf_op jit(solution)/shard_map/lookup_exchange/pallas_call | solution.py:201
  218.3 3.9 conditional.2
  219.9 2.3 multiply_reduce_fusion
  224.2 1.8 multiply_convert_fusion.hidden_ref
  226.1 6.7 %fusion.27.d_attn_ref = bf16[256,2048]{1,0:T(8,128)(2,1)} fusion(bf16[2048,4608]{1,0:T(8,128)(2,1)} %all-gather.2.cloned.1.call-done, bf16[1,256,2048]{2,1,0:T(8,128)(2,1)S(1)} %copy-done.3), kind=kOutput, calls=%fused_computation.48 | convolution fusion | flops 2148007936 | bytes 10485760 | tf_op jit(solution)/shard_map/lo,io->li/dot_general | solution.py:695
  232.8 8.3 %fusion.15.q_ref.k_ref.v_ref = f32[256,2560]{1,0:T(8,128)} fusion(bf16[256,2048]{1,0:T(8,128)(2,1)S(1)} %multiply_convert_fusion.hidden_ref, bf16[2048,4608]{1,0:T(8,128)(2,1)} %all-gather.2.cloned.1.call-done, f32[2560]{0:T(1024)S(1)} %maximum_convert_fusion), kind=kOutput, calls=%fused_computation.43 | convolution fusion | flops 2685009920 | bytes 14166016 | tf_op jit(solution)/shard_map/dot_general | solution.py:694
  241.2 19.4 %attention.1 = (bf16[256,2048]{1,0:T(8,128)(2,1)}, bf16[256,2048]{1,0:T(8,128)(2,1)}, bf16[256,256]{1,0:T(8,128)(2,1)}, bf16[256,256]{1,0:T(8,128)(2,1)}, f32[1,...) custom-call(f32[256,2560]{1,0:T(8,128)} %fusion.15.q_ref.k_ref.v_ref, f32[256,2560]{1,0:T(8,128)} %fusion.15.q_ref.k_ref.v_ref, ...), custom_call_target="tpu_custom_call" | custom-call | flops 1879048192 | bytes 10000000 | tf_op jit(solution)/shard_map/attention/pallas_call | solution.py:663
  260.6 8.1 %multiply_reduce_fusion.2 = (f32[2048]{0:T(1024)S(1)}, f32[256]{0:T(256)S(1)}, f32[256,2048]{1,0:T(8,128)S(1)}) fusion(f32[256,2048]{1,0:T(8,128)} %get-tuple-element.299, f32[256]{0:T(256)S(1)} %bitcast.62, f32[2048]{0:T(1024)S(1)} %reshape.248, bf16[2048,4608]{1,0:T(8,128)(2,1)} %all-gather.2.cloned.1.call-done, bf16[256,256]{1,0:T(8,128)(2,1)} %get-tuple-element.304, ...), kind=kOutput, calls=%fused_computation.52 | convolution fusion | flops 2691430144 | bytes 16009216 | tf_op jit(solution)/shard_map/lo,io->li/dot_general | solution.py:701
  268.7 2.2 add_convert_fusion
  271.0 1.3 convolution_convert_fusion.1.hot_send
  272.3 2.1 convolution_convert_fusion.cold_send
  280.0 1.5 pad_maximum_fusion.g_ref
  281.7 15.1 %weight_grads.1 = (f32[18,1024,256]{2,1,0:T(8,128)}, bf16[18,1024,256]{2,1,0:T(8,128)(2,1)S(1)}) custom-call(bf16[256,2048]{1,0:T(8,128)(2,1)S(1)} %multiply_convert_fusion.hidden_ref, bf16[256,2048]{1,0:T(8,128)(2,1)S(1)} %copy-done, bf16[256,4608]{1,0:T(8,128)(2,1)S(1)} %pad_maximum_fusion.g_ref), custom_call_target="tpu_custom_call" | custom-call | flops 4831838208 | bytes 28311552 | tf_op jit(solution)/shard_map/weight_grads/pallas_call | solution.py:510
  296.8 3.6 copy-done.2
  300.4 213.2 %return_exchange.1 = (bf16[5120,2048]{1,0:T(8,128)(2,1)}, f32[32,8,128]{2,1,0:T(8,128)}, f32[64,4608]{1,0:T(8,128)}) custom-call(bf16[160,2048]{1,0:T(8,128)(2,1)} %convolution_convert_fusion.1.hot_send, bf16[496,2048]{1,0:T(8,128)(2,1)} %convolution_convert_fusion.cold_send, f32[32,8,128]{2,1,0:T(8,128)} %bitcast.59, ...), custom_call_target="tpu_custom_call" | custom-call | flops 60000002048 | bytes 60000000 | tf_op jit(solution)/shard_map/return_exchange/pallas_call | solution.py:451
  515.8 1.5 fusion.59
  517.3 2.3 fusion.58
  519.6 79.4 %conditional.3 = (bf16[4748,2048]{1,0:T(8,128)(2,1)}) conditional(s32[]{:T(128)} %convert_element_type.96, (s32[32,160]{1,0:T(8,128)S(1)}, bf16[5120,2048]{1,0:T(8,128)(2,1)}) %tuple.116, (s32[]{:T(128)}, s32[32,256]{1,0:T(8,128)}, s32[]{:T(128)}, bf16[256,2048]{1,0:T(8,128)(2,1)S(1)}) %tuple.56), branch_computations={%region_14.18_spmd, %region_17.22_spmd} | conditional | flops 30000037888 | bytes 143479168 | solution.py:799
  521.6 77.4 %table_sum.1 = bf16[4748,2048]{1,0:T(8,128)(2,1)} custom-call(s32[10]{0:T(128)} %get-tuple-element.363.low_ref, s32[10]{0:T(128)} %get-tuple-element.362.high_ref, bf16[32,160,2048]{2,1,0:T(8,128)(2,1)} %bitcast.73, s32[10,1,512]{2,1,0:T(1,128)} %reshape.284.row_ref), custom_call_target="tpu_custom_call" | custom-call | flops 30000001024 | bytes 45000000 | tf_op jit(solution)/shard_map/cond/branch_0_fun/table_sum/pallas_call | solution.py:572
  599.0 7.3 %fusion.30 = bf16[1,256,2048]{2,1,0:T(8,128)(2,1)} fusion(f32[256,2048]{1,0:T(8,128)} %get-tuple-element.299, bf16[256,2048]{1,0:T(8,128)(2,1)S(1)} %copy-done.1, bf16[2048,4608]{1,0:T(8,128)(2,1)} %all-gather.2.cloned.1.call-done), kind=kOutput, calls=%fused_computation.49 | convolution fusion | flops 2148532224 | bytes 12582912 | tf_op jit(solution)/shard_map/dot_general | solution.py:697
  (84 shorter events, 23.4 us)
Async XLA Ops:
  7.2 218.9 %all-gather.2.cloned.1.call-start = ((), (), s32[]{:S(2)}) async-start(), calls=%async_computation | async-start | bytes 19464192 | tf_op jit(solution)/shard_map/all_gather | solution.py:722
  34.5 48.6 %copy-start.5 = (s32[32,160]{1,0:T(8,128)}, s32[32,160]{1,0:T(8,128)S(1)}, u32[]{:S(2)}) copy-start(s32[32,160]{1,0:T(8,128)S(1)} %select_reduce_fusion) | copy-start | bytes 61444
  35.2 47.9 %copy-start.13 = (s32[1,256]{1,0:T(1,128)S(1)}, s32[1,256]{1,0:T(1,128)}, u32[]{:S(2)}) copy-start(s32[1,256]{1,0:T(1,128)} %param.21) | copy-start | bytes 3076
  83.4 134.9 %copy-start.8 = (s32[256]{0:T(256)}, s32[256]{0:T(256)S(1)}, u32[]{:S(2)}) copy-start(s32[256]{0:T(256)S(1)} %get-tuple-element.379) | copy-start | bytes 3076
  218.3 1.6 copy-start.4
  222.9 3.2 copy-start.3
  268.7 2.3 copy-start.9
  271.0 4.0 copy-start.10
  271.0 4.6 copy-start.12
  271.0 5.3 copy-start.11
  272.3 7.7 %copy-start.7 = (bf16[256,256]{1,0:T(8,128)(2,1)S(1)}, bf16[256,256]{1,0:T(8,128)(2,1)}, u32[]{:S(2)}) copy-start(bf16[256,256]{1,0:T(8,128)(2,1)} %get-tuple-element.303) | copy-start | bytes 393220
  280.0 1.6 copy-start
  296.8 3.6 copy-start.2
  513.6 5.9 copy-start.6
  519.6 79.4 %copy-start.1 = (bf16[256,2048]{1,0:T(8,128)(2,1)S(1)}, bf16[256,2048]{1,0:T(8,128)(2,1)}, u32[]{:S(2)}) copy-start(bf16[256,2048]{1,0:T(8,128)(2,1)} %get-tuple-element.301.attn_ref) | copy-start | bytes 3145732
Sparse Core Ops, SparseCore 0:
  11.5 167.4 all-gather.1
where the time goes:
time: 610 us; the launch traced here: 613 us
  Pallas kernels  472 us (77%)
  local copies, waits for them, and re-layouts  65.6 us (11%)
  matrix products  36.6 us (6%)
  other arithmetic  22.8 us (4%)
  between operations  15.6 us (3%)
    pallas_call x1, Pallas kernels, return_exchange(): pl.pallas_call(return_kernel, out_shape=(jax.ShapeDtypeStruct((N_DEV * HO...  213 us
    pallas_call x1, Pallas kernels, lookup_exchange(): pl.pallas_call(lookup_kernel, out_shape=(jax.ShapeDtypeStruct((HOT_CAP, w...  135 us
    pallas_call x1, Pallas kernels, table_sum(): pl.pallas_call(table_sum_kernel, grid_spec=pltpu.PrefetchScalarGridSpec(n...  77.4 us
    gather x1, local copies, waits for them, and re-layouts, device_step(): jnp.take(table_part, jnp.maximum(rows, 0), axis=0, mode='clip')  47.9 us
    pallas_call x1, Pallas kernels, attention(): pl.pallas_call(attention_kernel, grid=(heads,), in_specs=[cols(own), cols...  19.4 us
    pallas_call x1, Pallas kernels, weight_grads(): pl.pallas_call(weight_grad_kernel, grid=(groups,), out_shape=(jax.ShapeDt...  15.1 us
    pallas_call x1, Pallas kernels, small_gather(): pl.pallas_call(small_gather_kernel, out_shape=jax.ShapeDtypeStruct((N_DEV...  12.6 us
  transfers between devices with their start and end apart: 1, of which 0 were waited for; matrix products, arithmetic and copies ran while one was open for 11% of the time, Pallas kernels for 24%

commit v1 on v0

--- a/solution.py
+++ b/solution.py
@@ -21,7 +21,7 @@
 
 RELAYS = {2: (26, 18, 10, 6), 4: (28, 20, 12, 14), 8: (30, 22)}
 N_RELAY = 4
-RELAY_STEPS = (6, 9, 12, 15)
+RELAY_STEPS = (8, 11, 14, 17)
 
 
 def far_blocks():
@@ -212,9 +212,19 @@
     )(send)
 
 
-def return_kernel(hot_send, cold_send, vec_send, own, oth, recv, vec_recv, out, relay,
-                  held, got0, send1, keep1, got1, send2, keep2, got2, send3, keep3, got3,
-                  held_sem, s0_sem, r0_sem, s1_sem, r1_sem, s2_sem, r2_sem, s3_sem, r3_sem, hs_sem, hr_sem, rr_sem, fs_sem, cs_sem, cr_sem, vs_sem, vr_sem, own_sem):
+GROUP = 256
+LAG = 4
+KEPT = LAG + 1
+
+
+def chunk_spot(dev):
+    z, y, x, core = dev // 8, dev // 4 % 2, dev // 2 % 2, dev % 2
+    return ((x * 2 + y) if core == 0 else (y * 2 + x)) * 4 + z
+
+
+def return_kernel(hot_send, cold_send, vec_send, hidden, attn, grads, recv, vec_recv, out, relay,
+                  held, oth, got0, send1, keep1, got1, send2, keep2, got2, send3, keep3, got3,
+                  s0_sem, r0_sem, s1_sem, r1_sem, s2_sem, r2_sem, s3_sem, r3_sem, hs_sem, hr_sem, rr_sem, fs_sem, cs_sem, cr_sem, vs_sem, vr_sem, own_sem):
     me = lax.axis_index("fsdp")
     enter_all(me)
 
@@ -285,7 +295,8 @@
     def _():
         own_cold.start()
 
-    groups, half, width = own.shape
+    groups, half, width = got0.shape
+    chunk = half // 16
     core, x, y, z = lax.rem(me, 2), lax.rem(me // 2, 2), lax.rem(me // 4, 2), me // 8
     first = jnp.where(core == 0, x, y)
     second = jnp.where(core == 0, y, x)
@@ -304,9 +315,6 @@
     def copy0(g):
         return to(oth.at[g], got0.at[g], s0_sem, r0_sem.at[g], me + 1 - 2 * core)
 
-    def load(g):
-        return pltpu.make_async_copy(own.at[g], held.at[lax.rem(g, 2)], held_sem.at[lax.rem(g, 2)])
-
     def copy1(g):
         return to(send1.at[g], got1.at[g], s1_sem, r1_sem.at[g], near1)
 
@@ -317,38 +325,48 @@
         peer = lax.rem(z + dz, 4)
         return to(send3.at[g, dz - 1], got3.at[g, dz - 1], s3_sem, r3_sem.at[g, dz - 1], me + 8 * (peer - z))
 
-    load(0).start()
-    load(1).start()
-
-    def start0(g, carry):
-        copy0(g).start()
-        return carry
-
-    lax.fori_loop(0, groups, start0, 0)
-
     def stage(lag, step, body):
         g = step - lag
 
         @pl.when((g >= 0) & (g < groups))
         def _():
-            body(g, lax.rem(g + 3, 3))
+            body(g, lax.rem(g, KEPT))
+
+    def make(g, slot):
+        def place(lhs):
+            cols = pl.ds(pl.multiple_of(g * width, width), width)
+            res = lax.dot_general(lhs[...], grads[:, cols], (((0,), (0,)), ((), ())), preferred_element_type=f32)
+            for mine in range(2):
+                @pl.when(core == mine)
+                def _(mine=mine):
+                    for dev in range(N_DEV):
+                        spot = chunk_spot(dev) * chunk
+                        piece = res[dev * chunk:(dev + 1) * chunk]
+                        if dev % 2 == mine:
+                            held[slot, spot:spot + chunk, :] = piece
+                        else:
+                            oth[g, spot:spot + chunk, :] = piece.astype(bf16)
+
+        @pl.when(g < groups * QKV // WCOLS)
+        def _():
+            place(hidden)
+
+        @pl.when(g >= groups * QKV // WCOLS)
+        def _():
+            place(attn)
+
+        copy0(g).start()
 
     def across_core(g, slot):
         copy0(g).wait_recv()
-        load(g).wait()
-        here = held.at[lax.rem(g, 2)]
         for sent in range(2):
             rows = part(half // 2, 1 - first if sent else first)
-            total = here[rows, :] + got0[g, rows, :].astype(f32)
+            total = held[slot, rows, :] + got0[g, rows, :].astype(f32)
             if sent:
                 send1[g] = total.astype(bf16)
             else:
                 keep1[slot] = total
         copy1(g).start()
-
-        @pl.when(g + 2 < groups)
-        def _():
-            load(g + 2).start()
 
     def across_first(g, slot):
         copy1(g).wait_recv()
@@ -382,10 +400,11 @@
         return to(relay.at[k], block(ends[k]), fs_sem.at[k], hr_sem.at[ends[k]], 0)
 
     def run(step, carry):
-        stage(0, step, across_core)
-        stage(2, step, across_first)
-        stage(4, step, across_second)
-        stage(6, step, across_z)
+        stage(0, step, make)
+        stage(2, step, across_core)
+        stage(2 + LAG, step, across_first)
+        stage(2 + 2 * LAG, step, across_second)
+        stage(2 + 3 * LAG, step, across_z)
 
         def pass_on(ends):
             for k in reversed(range(len(ends))):
@@ -397,7 +416,7 @@
         on_relays(me, pass_on)
         return carry
 
-    lax.fori_loop(0, groups + 6, run, 0)
+    lax.fori_loop(0, groups + 2 + 3 * LAG, run, 0)
 
     def passed(ends):
         for k in range(len(ends)):
@@ -442,88 +461,41 @@
         lax.fori_loop(1, N_DEV, arrived, 0)
 
 
-def return_exchange(hot_send, cold_send, vec_send, own, oth):
+def return_exchange(hot_send, cold_send, vec_send, hidden, attn, grads):
     width = hot_send.shape[1]
-    groups, half, cols = own.shape
+    tokens, rows = hidden.shape
+    cols, half, groups = GROUP, rows // 2, grads.shape[1] // GROUP
     dma = pltpu.SemaphoreType.DMA
     f32, bf16 = jnp.float32, jnp.bfloat16
     anywhere = pl.BlockSpec(memory_space=pl.ANY)
+    in_vmem = pl.BlockSpec(memory_space=pltpu.VMEM)
     return pl.pallas_call(
         return_kernel,
         out_shape=(jax.ShapeDtypeStruct((N_DEV * HOT_CAP, width), bf16),
                    jax.ShapeDtypeStruct(vec_send.shape, f32),
                    jax.ShapeDtypeStruct((half // 16, groups * cols), f32)),
-        in_specs=[anywhere] * 5,
-        out_specs=(anywhere, anywhere, pl.BlockSpec(memory_space=pltpu.VMEM)),
+        in_specs=[anywhere] * 3 + [in_vmem] * 3,
+        out_specs=(anywhere, anywhere, in_vmem),
         scratch_shapes=[pltpu.VMEM((N_RELAY, HOT_CAP, width), bf16),
-                        pltpu.VMEM((2, half, cols), f32), pltpu.VMEM((groups, half, cols), bf16),
-                        pltpu.VMEM((groups, half // 2, cols), bf16), pltpu.VMEM((3, half // 2, cols), f32),
+                        pltpu.VMEM((KEPT, half, cols), f32), pltpu.VMEM((groups, half, cols), bf16),
+                        pltpu.VMEM((groups, half, cols), bf16),
+                        pltpu.VMEM((groups, half // 2, cols), bf16), pltpu.VMEM((KEPT, half // 2, cols), f32),
                         pltpu.VMEM((groups, half // 2, cols), bf16),
-                        pltpu.VMEM((groups, half // 4, cols), bf16), pltpu.VMEM((3, half // 4, cols), f32),
+                        pltpu.VMEM((groups, half // 4, cols), bf16), pltpu.VMEM((KEPT, half // 4, cols), f32),
                         pltpu.VMEM((groups, half // 4, cols), bf16),
-                        pltpu.VMEM((groups, 3, half // 16, cols), bf16), pltpu.VMEM((3, half // 16, cols), f32),
+                        pltpu.VMEM((groups, 3, half // 16, cols), bf16), pltpu.VMEM((KEPT, half // 16, cols), f32),
                         pltpu.VMEM((groups, 3, half // 16, cols), bf16),
-                        dma((2,)), dma, dma((groups,)), dma, dma((groups,)), dma, dma((groups,)), dma, dma((groups, 3)),
+                        dma, dma((groups,)), dma, dma((groups,)), dma, dma((groups,)), dma, dma((groups, 3)),
                         dma, dma((N_DEV,)), dma((N_RELAY,)), dma((N_RELAY,)), dma((N_DEV,)), dma((N_DEV,)),
                         dma((N_DEV,)), dma((N_DEV,)), dma((3,))],
-        compiler_params=pltpu.CompilerParams(collective_id=3, has_side_effects=True, vmem_limit_bytes=56 * 1024 * 1024),
+        compiler_params=pltpu.CompilerParams(collective_id=3, has_side_effects=True, vmem_limit_bytes=60 * 1024 * 1024),
         cost_estimate=pl.CostEstimate(flops=60_000_000_000, bytes_accessed=60_000_000, transcendentals=0),
         name="return_exchange",
-    )(hot_send, cold_send, vec_send, own, oth)
-
-
-GROUP = 256
-CHUNK = 64
-
-
-def weight_grad_kernel(hidden_ref, attn_ref, g_ref, own_ref, oth_ref):
-    step = pl.program_id(0)
-    core = lax.rem(lax.axis_index("fsdp"), 2)
-    dims = (((0,), (0,)), ((), ()))
-
-    def place(lhs_ref):
-        res = lax.dot_general(lhs_ref[...], g_ref[...], dims, preferred_element_type=jnp.float32)
-        for mine in range(2):
-            @pl.when(core == mine)
-            def _(mine=mine):
-                for dev in range(N_DEV):
-                    z, y, x, c = dev // 8, dev // 4 % 2, dev // 2 % 2, dev % 2
-                    spot = ((x * 2 + y) if c == 0 else (y * 2 + x)) * 4 + z
-                    chunk = res[dev * CHUNK:(dev + 1) * CHUNK]
-                    if c == mine:
-                        own_ref[0, spot * CHUNK:(spot + 1) * CHUNK, :] = chunk
-                    else:
-                        oth_ref[0, spot * CHUNK:(spot + 1) * CHUNK, :] = chunk.astype(jnp.bfloat16)
-
-    @pl.when(step < QKV // GROUP)
-    def _():
-        place(hidden_ref)
-
-    @pl.when(step >= QKV // GROUP)
-    def _():
-        place(attn_ref)
-
-
-def weight_grads(hidden, attn_b, grads):
-    tokens, width = hidden.shape
-    groups, half = WCOLS // GROUP, width // 2
-    return pl.pallas_call(
-        weight_grad_kernel,
-        grid=(groups,),
-        out_shape=(jax.ShapeDtypeStruct((groups, half, GROUP), jnp.float32),
-                   jax.ShapeDtypeStruct((groups, half, GROUP), jnp.bfloat16)),
-        in_specs=[pl.BlockSpec((tokens, width), lambda j: (0, 0)),
-                  pl.BlockSpec((tokens, width), lambda j: (0, 0)),
-                  pl.BlockSpec((tokens, GROUP), lambda j: (0, j))],
-        out_specs=(pl.BlockSpec((1, half, GROUP), lambda j: (j, 0, 0)),) * 2,
-        compiler_params=pltpu.CompilerParams(vmem_limit_bytes=40 * 1024 * 1024),
-        cost_estimate=pl.CostEstimate(flops=2 * tokens * width * WCOLS, bytes_accessed=width * WCOLS * 3, transcendentals=0),
-        name="weight_grads",
-    )(hidden, attn_b, grads)
+    )(hot_send, cold_send, vec_send, hidden, attn, grads)
 
 
 SLOTS = 16
-TILE = 128
+TILE = 256
 
 
 def table_sum_kernel(low_ref, high_ref, dx_ref, row_ref, out_ref, total):
@@ -697,7 +669,7 @@
     proj_out = jnp.dot(attn_b, w_out, preferred_element_type=jnp.float32)
     block_out = (x_full + proj_out).astype(jnp.bfloat16)
     d_lin_b = jnp.concatenate([dq_b, dk_b, dv_b], axis=1)
-    grad_w = weight_grads(hidden, attn_b, jnp.concatenate([d_lin_b, grad_out], axis=1))
+    grad_w = (hidden, attn_b, jnp.concatenate([d_lin_b, grad_out], axis=1))
     d_hidden = jnp.einsum("lo,io->li", d_lin_b, w_qkv, preferred_element_type=jnp.float32)
     grad_gain = jnp.sum(d_hidden * x_norm, axis=0)
     d_norm = d_hidden * gain_f

time: 610 us -> 555 us (0.910)
  Pallas kernels: 472 us -> 419 us
    pallas_call x1, Pallas kernels: 213 us -> 190 us  [return_exchange(): pl.pallas_call(return_kernel, out_shape=(jax.ShapeDtypeStruct((N_DEV * HO...]
    pallas_call x1, Pallas kernels: 77.4 us -> 61.2 us  [table_sum(): pl.pallas_call(table_sum_kernel, grid_spec=pltpu.PrefetchScalarGridSpec(n...]
    pallas_call x1 -> x0, Pallas kernels: 15.1 us -> none  [weight_grads(): pl.pallas_call(weight_grad_kernel, grid=(groups,), out_shape=(jax.ShapeDt...]
  transfers between devices with their start and end apart: 1 -> 1, of which waited for: 0 -> 0; matrix products, arithmetic and copies ran while one was open for 11% -> 12% of each run, Pallas kernels for 24% -> 27%
where the time goes in v1:
time: 555 us; the launch traced here: 554 us
  Pallas kernels  419 us (75%)
  local copies, waits for them, and re-layouts  60.4 us (11%)
  matrix products  37 us (7%)
  other arithmetic  22.6 us (4%)
  between operations  15.7 us (3%)
    pallas_call x1, Pallas kernels, return_exchange(): pl.pallas_call(return_kernel, out_shape=(jax.ShapeDtypeStruct((N_DEV * HO...  190 us
    pallas_call x1, Pallas kernels, lookup_exchange(): pl.pallas_call(lookup_kernel, out_shape=(jax.ShapeDtypeStruct((HOT_CAP, w...  136 us
    pallas_call x1, Pallas kernels, table_sum(): pl.pallas_call(table_sum_kernel, grid_spec=pltpu.PrefetchScalarGridSpec(n...  61.2 us
    gather x1, local copies, waits for them, and re-layouts, device_step(): jnp.take(table_part, jnp.maximum(rows, 0), axis=0, mode='clip')  47.9 us
    pallas_call x1, Pallas kernels, attention(): pl.pallas_call(attention_kernel, grid=(heads,), in_specs=[cols(own), cols...  19.4 us
    pallas_call x1, Pallas kernels, small_gather(): pl.pallas_call(small_gather_kernel, out_shape=jax.ShapeDtypeStruct((N_DEV...  12.6 us
  transfers between devices with their start and end apart: 1, of which 0 were waited for; matrix products, arithmetic and copies ran while one was open for 12% of the time, Pallas kernels for 27%

profile of v1, /device:TPU:0, one launch (start us, length us, event | category | flops | bytes accessed | tf_op | source)
XLA Modules:
  0.0 554.2 jit_solution(4669422858336385806)
XLA Ops:
  7.2 1.9 pad_maximum_fusion.1
  11.3 12.6 %small_gather.1 = f32[32,8,128]{2,1,0:T(8,128)} custom-call(f32[8,128]{1,0:T(8,128)} %maximum_bitcast_fusion.src), custom_call_target="tpu_custom_call" | custom-call | tf_op jit(solution)/shard_map/small_gather/pallas_call | solution.py:76
  29.6 2.6 convert_reduce_fusion
  32.2 1.2 select_reduce_fusion
  34.2 47.9 %gather_fusion.1 = bf16[5120,2048]{1,0:T(8,128)(2,1)} fusion(bf16[4748,2048]{1,0:T(8,128)(2,1)} %param.23, s32[5120]{0:T(1024)S(1)} %broadcast_clamp_fusion), kind=kCustom, calls=%fused_computation.1 | custom fusion | bytes 41963520 | tf_op jit(solution)/shard_map/jit(_take)/gather | solution.py:713
  82.6 135.7 %lookup_exchange.1 = (bf16[160,2048]{1,0:T(8,128)(2,1)S(1)}, bf16[496,2048]{1,0:T(8,128)(2,1)S(1)}) custom-call(bf16[5120,2048]{1,0:T(8,128)(2,1)} %gather_fusion.1), custom_call_target="tpu_custom_call" | custom-call | flops 60000002048 | bytes 30000000 | tf_op jit(solution)/shard_map/lookup_exchange/pallas_call | solution.py:201
  218.3 2.7 conditional.2
  218.8 2.3 multiply_reduce_fusion
  222.4 1.8 multiply_convert_fusion.hidden
  224.3 7.1 %fusion.27.d_attn_ref = bf16[256,2048]{1,0:T(8,128)(2,1)} fusion(bf16[2048,4608]{1,0:T(8,128)(2,1)} %all-gather.2.cloned.1.call-done, bf16[1,256,2048]{2,1,0:T(8,128)(2,1)S(1)} %copy-done), kind=kOutput, calls=%fused_computation.48 | convolution fusion | flops 2148007936 | bytes 10485760 | tf_op jit(solution)/shard_map/lo,io->li/dot_general | solution.py:667
  231.4 8.3 %fusion.15.q_ref.k_ref.v_ref = f32[256,2560]{1,0:T(8,128)} fusion(bf16[256,2048]{1,0:T(8,128)(2,1)S(1)} %multiply_convert_fusion.hidden, bf16[2048,4608]{1,0:T(8,128)(2,1)} %all-gather.2.cloned.1.call-done, f32[2560]{0:T(1024)S(1)} %maximum_convert_fusion), kind=kOutput, calls=%fused_computation.43 | convolution fusion | flops 2685009920 | bytes 14166016 | tf_op jit(solution)/shard_map/dot_general | solution.py:666
  239.7 19.4 %attention.1 = (bf16[256,2048]{1,0:T(8,128)(2,1)}, bf16[256,2048]{1,0:T(8,128)(2,1)}, bf16[256,256]{1,0:T(8,128)(2,1)}, bf16[256,256]{1,0:T(8,128)(2,1)}, f32[1,...) custom-call(f32[256,2560]{1,0:T(8,128)} %fusion.15.q_ref.k_ref.v_ref, f32[256,2560]{1,0:T(8,128)} %fusion.15.q_ref.k_ref.v_ref, ...), custom_call_target="tpu_custom_call" | custom-call | flops 1879048192 | bytes 10000000 | tf_op jit(solution)/shard_map/attention/pallas_call | solution.py:635
  259.1 8.1 %multiply_reduce_fusion.2 = (f32[2048]{0:T(1024)S(1)}, f32[256]{0:T(256)S(1)}, f32[256,2048]{1,0:T(8,128)S(1)}) fusion(f32[256,2048]{1,0:T(8,128)} %get-tuple-element.297, f32[256]{0:T(256)S(1)} %bitcast.62, f32[2048]{0:T(1024)S(1)} %reshape.248, bf16[2048,4608]{1,0:T(8,128)(2,1)} %all-gather.2.cloned.1.call-done, bf16[256,256]{1,0:T(8,128)(2,1)} %get-tuple-element.302, ...), kind=kOutput, calls=%fused_computation.52 | convolution fusion | flops 2691430144 | bytes 16009216 | tf_op jit(solution)/shard_map/lo,io->li/dot_general | solution.py:673
  267.2 2.2 add_convert_fusion
  269.5 1.3 convolution_convert_fusion.1.hot_send
  270.8 2.1 convolution_convert_fusion.cold_send
  278.6 2.6 pad_maximum_fusion.grads
  281.2 189.6 %return_exchange.1 = (bf16[5120,2048]{1,0:T(8,128)(2,1)}, f32[32,8,128]{2,1,0:T(8,128)}, f32[64,4608]{1,0:T(8,128)}) custom-call(bf16[160,2048]{1,0:T(8,128)(2,1)} %convolution_convert_fusion.1.hot_send, bf16[496,2048]{1,0:T(8,128)(2,1)} %convolution_convert_fusion.cold_send, f32[32,8,128]{2,1,0:T(8,128)} %bitcast.59, bf16[256,2048]{1,0:T(8,128)(2,1)} %copy-done.1, ...), custom_call_target="tpu_custom_call" | custom-call | flops 60000002048 | bytes 60000000 | tf_op jit(solution)/shard_map/return_exchange/pallas_call | solution.py:472
  470.9 0.9 reduce_sum.91
  473.0 1.5 fusion.59
  474.5 2.3 fusion.58
  476.8 63.2 %conditional.3 = (bf16[4748,2048]{1,0:T(8,128)(2,1)}) conditional(s32[]{:T(128)} %convert_element_type.96, (s32[32,160]{1,0:T(8,128)S(1)}, bf16[5120,2048]{1,0:T(8,128)(2,1)}) %tuple.116, (s32[]{:T(128)}, s32[32,256]{1,0:T(8,128)}, s32[]{:T(128)}, bf16[256,2048]{1,0:T(8,128)(2,1)S(1)}) %tuple.117), branch_computations={%region_14.18_spmd, %region_17.22_spmd} | conditional | flops 30000037888 | bytes 143479168 | solution.py:771
  478.8 61.2 %table_sum.1 = bf16[4748,2048]{1,0:T(8,128)(2,1)} custom-call(s32[10]{0:T(128)} %get-tuple-element.359.low_ref, s32[10]{0:T(128)} %get-tuple-element.358.high_ref, bf16[32,160,2048]{2,1,0:T(8,128)(2,1)} %bitcast.73, s32[10,1,512]{2,1,0:T(1,128)} %reshape.284.row_ref), custom_call_target="tpu_custom_call" | custom-call | flops 30000001024 | bytes 45000000 | tf_op jit(solution)/shard_map/cond/branch_0_fun/table_sum/pallas_call | solution.py:544
  540.0 7.3 %fusion.30 = bf16[1,256,2048]{2,1,0:T(8,128)(2,1)} fusion(f32[256,2048]{1,0:T(8,128)} %get-tuple-element.297, bf16[256,2048]{1,0:T(8,128)(2,1)S(1)} %copy-done.11, bf16[2048,4608]{1,0:T(8,128)(2,1)} %all-gather.2.cloned.1.call-done), kind=kOutput, calls=%fused_computation.49 | convolution fusion | flops 2148532224 | bytes 12582912 | tf_op jit(solution)/shard_map/dot_general | solution.py:669
  (79 shorter events, 18.4 us)
Async XLA Ops:
  7.2 217.1 %all-gather.2.cloned.1.call-start = ((), (), s32[]{:S(2)}) async-start(), calls=%async_computation | async-start | bytes 19464192 | tf_op jit(solution)/shard_map/all_gather | solution.py:694
  33.5 0.6 copy-start.3
  34.2 184.1 %copy-start.6 = (s32[32,256]{1,0:T(8,128)}, s32[32,256]{1,0:T(8,128)S(1)}, u32[]{:S(2)}) copy-start(s32[32,256]{1,0:T(8,128)S(1)} %slice_convert_fusion) | copy-start | bytes 98308
  34.2 47.9 %copy-start.10 = (s32[1,256]{1,0:T(1,128)S(1)}, s32[1,256]{1,0:T(1,128)}, u32[]{:S(2)}) copy-start(s32[1,256]{1,0:T(1,128)} %param.21) | copy-start | bytes 3076
  221.0 3.2 copy-start
  224.3 7.1 %copy-start.1 = (bf16[256,2048]{1,0:T(8,128)(2,1)}, bf16[256,2048]{1,0:T(8,128)(2,1)S(1)}, u32[]{:S(2)}) copy-start(bf16[256,2048]{1,0:T(8,128)(2,1)S(1)} %multiply_convert_fusion.hidden) | copy-start | bytes 3145732
  269.5 4.0 copy-start.7
  269.5 4.6 copy-start.9
  269.5 5.3 copy-start.8
  270.8 7.8 %copy-start.2 = (bf16[256,2048]{1,0:T(8,128)(2,1)S(1)}, bf16[256,2048]{1,0:T(8,128)(2,1)}, u32[]{:S(2)}) copy-start(bf16[256,2048]{1,0:T(8,128)(2,1)} %get-tuple-element.300) | copy-start | bytes 3145732
  270.8 7.8 %copy-start.5 = (bf16[256,256]{1,0:T(8,128)(2,1)S(1)}, bf16[256,256]{1,0:T(8,128)(2,1)}, u32[]{:S(2)}) copy-start(bf16[256,256]{1,0:T(8,128)(2,1)} %get-tuple-element.301) | copy-start | bytes 393220
  470.9 5.9 %copy-start.4 = (s32[32,160]{1,0:T(8,128)S(1)}, s32[32,160]{1,0:T(8,128)}, u32[]{:S(2)}) copy-start(s32[32,160]{1,0:T(8,128)} %copy-done.3) | copy-start | bytes 61444
  476.8 63.2 %copy-start.11 = (bf16[256,2048]{1,0:T(8,128)(2,1)S(1)}, bf16[256,2048]{1,0:T(8,128)(2,1)}, u32[]{:S(2)}) copy-start(bf16[256,2048]{1,0:T(8,128)(2,1)} %get-tuple-element.299.attn) | copy-start | bytes 3145732
Sparse Core Ops, SparseCore 0:
  11.5 167.9 all-gather.1

commit v2 on v1

--- a/solution.py
+++ b/solution.py
@@ -19,18 +19,13 @@
 MESH = pl.DeviceIdType.MESH
 
 
-RELAYS = {2: (26, 18, 10, 6), 4: (28, 20, 12, 14), 8: (30, 22)}
+RELAYS = {2: (26, 18, 10, 6), 3: (27, 19, 11), 4: (28, 20, 12), 5: (29, 21, 13, 7), 8: (30, 22, 14), 9: (31, 23, 15)}
 N_RELAY = 4
-RELAY_STEPS = (8, 11, 14, 17)
+RELAY_STEPS = (6, 9, 12, 15)
 
 
 def far_blocks():
-    out = []
-    for k in range(N_RELAY):
-        for via, ends in RELAYS.items():
-            if k < len(ends):
-                out.extend((ends[k] + core, via + core, k) for core in range(2))
-    return out
+    return [(ends[k], via, k) for k in range(N_RELAY) for via, ends in RELAYS.items() if k < len(ends)]
 
 
 def near_blocks():
@@ -90,10 +85,9 @@
 
 def on_relays(me, body):
     for via, ends in RELAYS.items():
-        for core in range(2):
-            @pl.when(me == via + core)
-            def _(ends=ends, core=core):
-                body([end + core for end in ends])
+        @pl.when(me == via)
+        def _(ends=ends):
+            body(ends)
 
 
 def lookup_kernel(send, hot_recv, cold_recv, relay, hs_sem, hr_sem, rr_sem, fs_sem, cs_sem, cr_sem, own_sem):
@@ -222,8 +216,8 @@
     return ((x * 2 + y) if core == 0 else (y * 2 + x)) * 4 + z
 
 
-def return_kernel(hot_send, cold_send, vec_send, hidden, attn, grads, recv, vec_recv, out, relay,
-                  held, oth, got0, send1, keep1, got1, send2, keep2, got2, send3, keep3, got3,
+def return_kernel(hot_send, cold_send, vec_send, w_all, hidden, attn, grads, x_rows, recv, vec_recv, out, block_out, relay,
+                  w_tile, w_sem, held, oth, got0, send1, keep1, got1, send2, keep2, got2, send3, keep3, got3,
                   s0_sem, r0_sem, s1_sem, r1_sem, s2_sem, r2_sem, s3_sem, r3_sem, hs_sem, hr_sem, rr_sem, fs_sem, cs_sem, cr_sem, vs_sem, vr_sem, own_sem):
     me = lax.axis_index("fsdp")
     enter_all(me)
@@ -396,6 +390,25 @@
             total = total + got3[g, dz - 1].astype(f32)
         out[:, pl.ds(pl.multiple_of(g * width, width), width)] = total
 
+    out_tiles = block_out.shape[1] // width
+
+    def fetch(j):
+        cols = pl.ds(pl.multiple_of(QKV + j * width, width), width)
+        return pltpu.make_async_copy(w_all.at[:, cols], w_tile.at[lax.rem(j, 2)], w_sem.at[lax.rem(j, 2)])
+
+    def project(j, slot):
+        fetch(j).wait()
+        cols = pl.ds(pl.multiple_of(j * width, width), width)
+        proj = jnp.dot(attn[...], w_tile[lax.rem(j, 2)], preferred_element_type=f32)
+        block_out[:, cols] = (x_rows[:, cols].astype(f32) + proj).astype(bf16)
+
+        @pl.when(j + 2 < out_tiles)
+        def _():
+            fetch(j + 2).start()
+
+    fetch(0).start()
+    fetch(1).start()
+
     def onward(ends, k):
         return to(relay.at[k], block(ends[k]), fs_sem.at[k], hr_sem.at[ends[k]], 0)
 
@@ -406,6 +419,10 @@
         stage(2 + 2 * LAG, step, across_second)
         stage(2 + 3 * LAG, step, across_z)
 
+        @pl.when((step >= 4) & (step < 4 + out_tiles))
+        def _():
+            project(step - 4, 0)
+
         def pass_on(ends):
             for k in reversed(range(len(ends))):
                 @pl.when(step == RELAY_STEPS[N_RELAY - 1 - k])
@@ -461,7 +478,7 @@
         lax.fori_loop(1, N_DEV, arrived, 0)
 
 
-def return_exchange(hot_send, cold_send, vec_send, hidden, attn, grads):
+def return_exchange(hot_send, cold_send, vec_send, w_all, hidden, attn, grads, x_rows):
     width = hot_send.shape[1]
     tokens, rows = hidden.shape
     cols, half, groups = GROUP, rows // 2, grads.shape[1] // GROUP
@@ -473,10 +490,12 @@
         return_kernel,
         out_shape=(jax.ShapeDtypeStruct((N_DEV * HOT_CAP, width), bf16),
                    jax.ShapeDtypeStruct(vec_send.shape, f32),
-                   jax.ShapeDtypeStruct((half // 16, groups * cols), f32)),
-        in_specs=[anywhere] * 3 + [in_vmem] * 3,
-        out_specs=(anywhere, anywhere, in_vmem),
+                   jax.ShapeDtypeStruct((half // 16, groups * cols), f32),
+                   jax.ShapeDtypeStruct(x_rows.shape, bf16)),
+        in_specs=[anywhere] * 4 + [in_vmem] * 4,
+        out_specs=(anywhere, anywhere, in_vmem, in_vmem),
         scratch_shapes=[pltpu.VMEM((N_RELAY, HOT_CAP, width), bf16),
+                        pltpu.VMEM((2, rows, cols), bf16), dma((2,)),
                         pltpu.VMEM((KEPT, half, cols), f32), pltpu.VMEM((groups, half, cols), bf16),
                         pltpu.VMEM((groups, half, cols), bf16),
                         pltpu.VMEM((groups, half // 2, cols), bf16), pltpu.VMEM((KEPT, half // 2, cols), f32),
@@ -491,7 +510,7 @@
         compiler_params=pltpu.CompilerParams(collective_id=3, has_side_effects=True, vmem_limit_bytes=60 * 1024 * 1024),
         cost_estimate=pl.CostEstimate(flops=60_000_000_000, bytes_accessed=60_000_000, transcendentals=0),
         name="return_exchange",
-    )(hot_send, cold_send, vec_send, hidden, attn, grads)
+    )(hot_send, cold_send, vec_send, w_all, hidden, attn, grads, x_rows)
 
 
 SLOTS = 16
@@ -584,22 +603,28 @@
 
     q_lin = q_ref[...]
     q_rot = (q_lin * cos_t + turn(q_lin) * sin_t).astype(jnp.bfloat16)
-    scores = lax.dot_general(q_rot, k_rot[...], rows_t, preferred_element_type=f32) * scale
-    seq = scores.shape[0]
-    causal = lax.broadcasted_iota(jnp.int32, (seq, seq), 0) >= lax.broadcasted_iota(jnp.int32, (seq, seq), 1)
-    scores = jnp.where(causal, scores, MASK_VALUE)
-    weight = jnp.exp(scores - jnp.max(scores, axis=1, keepdims=True))
-    prob_f = weight / jnp.sum(weight, axis=1, keepdims=True)
-    prob_b = prob_f.astype(jnp.bfloat16)
-    attn_ref[...] = jnp.dot(prob_b, v_val[...], preferred_element_type=f32).astype(jnp.bfloat16)
-
-    d_attn = d_attn_ref[...]
-    d_probs = lax.dot_general(d_attn, v_val[...], rows_t, preferred_element_type=f32)
-    dv_sum[...] += lax.dot_general(prob_b, d_attn, cols_t, preferred_element_type=f32)
-    d_scores = prob_f * (d_probs - jnp.sum(d_probs * prob_f, axis=1, keepdims=True))
-    d_scores = (d_scores * scale).astype(jnp.bfloat16)
-    d_qrot = jnp.dot(d_scores, k_rot[...], preferred_element_type=f32)
-    dk_sum[...] += lax.dot_general(d_scores, q_rot, cols_t, preferred_element_type=f32)
+    seq = q_lin.shape[0]
+    part = seq // 2
+    d_qrot = []
+    for low in (0, part):
+        seen = low + part
+        at, keys = slice(low, seen), slice(0, seen)
+        scores = lax.dot_general(q_rot[at], k_rot[keys], rows_t, preferred_element_type=f32) * scale
+        causal = low + lax.broadcasted_iota(jnp.int32, (part, seen), 0) >= lax.broadcasted_iota(jnp.int32, (part, seen), 1)
+        scores = jnp.where(causal, scores, MASK_VALUE)
+        weight = jnp.exp(scores - jnp.max(scores, axis=1, keepdims=True))
+        prob_f = weight * (1.0 / jnp.sum(weight, axis=1, keepdims=True))
+        prob_b = prob_f.astype(jnp.bfloat16)
+        attn_ref[at] = jnp.dot(prob_b, v_val[keys], preferred_element_type=f32).astype(jnp.bfloat16)
+
+        d_attn = d_attn_ref[at]
+        d_probs = lax.dot_general(d_attn, v_val[keys], rows_t, preferred_element_type=f32)
+        dv_sum[keys] += lax.dot_general(prob_b, d_attn, cols_t, preferred_element_type=f32)
+        d_scores = prob_f * (d_probs - jnp.sum(d_probs * prob_f, axis=1, keepdims=True))
+        d_scores = (d_scores * scale).astype(jnp.bfloat16)
+        d_qrot.append(jnp.dot(d_scores, k_rot[keys], preferred_element_type=f32))
+        dk_sum[keys] += lax.dot_general(d_scores, q_rot[at], cols_t, preferred_element_type=f32)
+    d_qrot = jnp.concatenate(d_qrot, axis=0)
     d_query = d_qrot * cos_t - turn(d_qrot) * sin_t
     dq_ref[...] = d_query.astype(jnp.bfloat16)
     gq_ref[...] = jnp.sum(d_query, axis=0, keepdims=True)
@@ -666,16 +691,14 @@
     lin = jnp.dot(hidden, w_qkv, preferred_element_type=jnp.float32) + b_qkv.astype(jnp.float32)
     d_attn = jnp.einsum("lo,io->li", grad_out, w_out, preferred_element_type=jnp.float32).astype(jnp.bfloat16)
     attn_b, dq_b, dk_b, dv_b, grad_bq, grad_bk, grad_bv = attention(lin, d_attn, cos_t, sin_t)
-    proj_out = jnp.dot(attn_b, w_out, preferred_element_type=jnp.float32)
-    block_out = (x_full + proj_out).astype(jnp.bfloat16)
     d_lin_b = jnp.concatenate([dq_b, dk_b, dv_b], axis=1)
-    grad_w = (hidden, attn_b, jnp.concatenate([d_lin_b, grad_out], axis=1))
+    grad_in = (hidden, attn_b, jnp.concatenate([d_lin_b, grad_out], axis=1))
     d_hidden = jnp.einsum("lo,io->li", d_lin_b, w_qkv, preferred_element_type=jnp.float32)
     grad_gain = jnp.sum(d_hidden * x_norm, axis=0)
     d_norm = d_hidden * gain_f
     d_x = grad_out.astype(jnp.float32) + inv_rms * (d_norm - x_norm * jnp.mean(d_norm * x_norm, axis=-1, keepdims=True))
     grad_b = jnp.concatenate([grad_bq[0], grad_bk[0], grad_bv[0]])
-    return block_out, d_x, grad_w, grad_gain, grad_b
+    return d_x, grad_in, grad_gain, grad_b
 
 
 def solution(mesh):
@@ -744,7 +767,7 @@
 
         x_rows = lax.cond(overflow, rows_ring, rows_fast)
         g_rows = grad_out.reshape(seq_len, model_width)
-        block_out, d_x, grad_w, grad_gain, grad_b = block_fwd_bwd(x_rows, g_rows, gain_full, w_all, b_qkv)
+        d_x, grad_in, grad_gain, grad_b = block_fwd_bwd(x_rows, g_rows, gain_full, w_all, b_qkv)
         dx_b = d_x.astype(jnp.bfloat16)
         tdims = (((0,), (0,)), ((), ()))
         hot_back = lax.dot_general(hot_pick, dx_b, tdims, preferred_element_type=jnp.float32).astype(jnp.bfloat16)
@@ -752,7 +775,8 @@
         vec_grad = jnp.concatenate(
             [grad_gain.reshape(N_DEV, 64), grad_b[:2048].reshape(N_DEV, 64), grad_b[2048:2304].reshape(N_DEV, 8),
              grad_b[2304:].reshape(N_DEV, 8), jnp.zeros((N_DEV, 1024 - 144), jnp.float32)], axis=1)
-        dx_recv, vec_sum, w_red = return_exchange(hot_back, cold_back, vec_grad.reshape(N_DEV, 8, 128), *grad_w)
+        dx_recv, vec_sum, w_red, block_out = return_exchange(
+            hot_back, cold_back, vec_grad.reshape(N_DEV, 8, 128), w_all, *grad_in, x_rows)
 
         def table_fast():
             return table_sum(dx_recv, rows, rows_dev)

time: 555 us -> 554 us (level)
  matrix products: 37 us -> 27.1 us
  Pallas kernels: 419 us -> 426 us
    pallas_call x1, Pallas kernels: 136 us -> 150 us  [lookup_exchange(): pl.pallas_call(lookup_kernel, out_shape=(jax.ShapeDtypeStruct((HOT_CAP, w...]
    pallas_call x1, Pallas kernels: 190 us -> 176 us  [return_exchange(): pl.pallas_call(return_kernel, out_shape=(jax.ShapeDtypeStruct((N_DEV * HO...]
    pallas_call x1, Pallas kernels: 19.4 us -> 27 us  [attention(): pl.pallas_call(attention_kernel, grid=(heads,), in_specs=[cols(own), cols...]
    dot_general x1 -> x0, matrix products: 7.34 us -> none  [block_fwd_bwd(): proj_out = jnp.dot(attn_b, w_out, preferred_element_type=jnp.float32)]
  transfers between devices with their start and end apart: 1 -> 1, of which waited for: 0 -> 0; matrix products, arithmetic and copies ran while one was open for 12% -> 11% of each run, Pallas kernels for 27% -> 29%
where the time goes in v2:
time: 554 us; the launch traced here: 550 us
  Pallas kernels  426 us (77%)
  local copies, waits for them, and re-layouts  61.7 us (11%)
  matrix products  27.1 us (5%)
  other arithmetic  19.4 us (4%)
  between operations  15.7 us (3%)
    pallas_call x1, Pallas kernels, return_exchange(): pl.pallas_call(return_kernel, out_shape=(jax.ShapeDtypeStruct((N_DEV * HO...  176 us
    pallas_call x1, Pallas kernels, lookup_exchange(): pl.pallas_call(lookup_kernel, out_shape=(jax.ShapeDtypeStruct((HOT_CAP, w...  150 us
    pallas_call x1, Pallas kernels, table_sum(): pl.pallas_call(table_sum_kernel, grid_spec=pltpu.PrefetchScalarGridSpec(n...  60.5 us
    gather x1, local copies, waits for them, and re-layouts, device_step(): jnp.take(table_part, jnp.maximum(rows, 0), axis=0, mode='clip')  47.9 us
    pallas_call x1, Pallas kernels, attention(): pl.pallas_call(attention_kernel, grid=(heads,), in_specs=[cols(own), cols...  27 us
    pallas_call x1, Pallas kernels, small_gather(): pl.pallas_call(small_gather_kernel, out_shape=jax.ShapeDtypeStruct((N_DEV...  12.6 us
  transfers between devices with their start and end apart: 1, of which 0 were waited for; matrix products, arithmetic and copies ran while one was open for 11% of the time, Pallas kernels for 29%

profile of v2, /device:TPU:0, one launch (start us, length us, event | category | flops | bytes accessed | tf_op | source)
XLA Modules:
  0.0 550.3 jit_solution(1839745085739749927)
XLA Ops:
  7.2 1.9 pad_maximum_fusion.1
  11.3 12.6 %small_gather.1 = f32[32,8,128]{2,1,0:T(8,128)} custom-call(f32[8,128]{1,0:T(8,128)} %maximum_bitcast_fusion.src), custom_call_target="tpu_custom_call" | custom-call | tf_op jit(solution)/shard_map/small_gather/pallas_call | solution.py:71
  23.9 0.9 copy.43
  24.8 0.9 copy.42
  29.6 2.6 convert_reduce_fusion
  32.2 1.2 select_reduce_fusion
  34.2 47.9 %gather_fusion.1 = bf16[5120,2048]{1,0:T(8,128)(2,1)} fusion(bf16[4748,2048]{1,0:T(8,128)(2,1)} %param.23, s32[5120]{0:T(1024)S(1)} %broadcast_clamp_fusion), kind=kCustom, calls=%fused_computation.1 | custom fusion | bytes 41963520 | tf_op jit(solution)/shard_map/jit(_take)/gather | solution.py:736
  82.6 149.7 %lookup_exchange.1 = (bf16[160,2048]{1,0:T(8,128)(2,1)S(1)}, bf16[496,2048]{1,0:T(8,128)(2,1)S(1)}) custom-call(bf16[5120,2048]{1,0:T(8,128)(2,1)} %gather_fusion.1), custom_call_target="tpu_custom_call" | custom-call | flops 60000002048 | bytes 30000000 | tf_op jit(solution)/shard_map/lookup_exchange/pallas_call | solution.py:195
  232.4 2.2 conditional.2
  232.8 1.8 multiply_reduce_fusion
  236.6 6.7 %fusion.18.d_attn_ref = bf16[256,2048]{1,0:T(8,128)(2,1)} fusion(bf16[2048,4608]{1,0:T(8,128)(2,1)} %all-gather.2.cloned.1.call-done.w_all, bf16[1,256,2048]{2,1,0:T(8,128)(2,1)S(1)} %copy-done.3), kind=kOutput, calls=%fused_computation.43 | convolution fusion | flops 2148007936 | bytes 10485760 | tf_op jit(solution)/shard_map/lo,io->li/dot_general | solution.py:692
  243.4 8.3 %fusion.12.q_ref.k_ref.v_ref = f32[256,2560]{1,0:T(8,128)} fusion(bf16[256,2048]{1,0:T(8,128)(2,1)S(1)} %multiply_convert_fusion.hidden, bf16[2048,4608]{1,0:T(8,128)(2,1)} %all-gather.2.cloned.1.call-done.w_all, f32[2560]{0:T(1024)S(1)} %maximum_convert_fusion), kind=kOutput, calls=%fused_computation.40 | convolution fusion | flops 2685009920 | bytes 14166016 | tf_op jit(solution)/shard_map/dot_general | solution.py:691
  251.7 27.0 %attention.1 = (bf16[256,2048]{1,0:T(8,128)(2,1)}, bf16[256,2048]{1,0:T(8,128)(2,1)}, bf16[256,256]{1,0:T(8,128)(2,1)}, bf16[256,256]{1,0:T(8,128)(2,1)}, f32[1,...) custom-call(f32[256,2560]{1,0:T(8,128)} %fusion.12.q_ref.k_ref.v_ref, f32[256,2560]{1,0:T(8,128)} %fusion.12.q_ref.k_ref.v_ref, ...), custom_call_target="tpu_custom_call" | custom-call | flops 1879048192 | bytes 10000000 | tf_op jit(solution)/shard_map/attention/pallas_call | solution.py:660
  278.7 6.4 %multiply_reduce_fusion.2 = (f32[2048]{0:T(1024)S(1)}, f32[256]{0:T(256)S(1)}, f32[256,2048]{1,0:T(8,128)S(1)}) fusion(f32[256,2048]{1,0:T(8,128)S(1)} %copy-done.1, f32[256]{0:T(256)S(1)} %bitcast.61, f32[2048]{0:T(1024)S(1)} %reshape.248, bf16[2048,4608]{1,0:T(8,128)(2,1)} %all-gather.2.cloned.1.call-done.w_all, bf16[256,256]{1,0:T(8,128)(2,1)} %get-tuple-element.303, ...), kind=kOutput, calls=%fused_computation.46 | convolution fusion | flops 2691430144 | bytes 16009216 | tf_op jit(solution)/shard_map/lo,io->li/dot_general | solution.py:696
  285.9 1.3 convolution_convert_fusion.1.hot_send
  287.2 2.1 convolution_convert_fusion.cold_send
  295.0 2.6 pad_maximum_fusion.grads
  297.6 176.5 %return_exchange.1 = (bf16[5120,2048]{1,0:T(8,128)(2,1)}, f32[32,8,128]{2,1,0:T(8,128)}, f32[64,4608]{1,0:T(8,128)}, bf16[256,2048]{1,0:T(8,128)(2,1)}) custom-call(bf16[160,2048]{1,0:T(8,128)(2,1)} %convolution_convert_fusion.1.hot_send, bf16[496,2048]{1,0:T(8,128)(2,1)} %convolution_convert_fusion.cold_send, f32[32,8,128]{2,1,0:T(8,128)} %bitcast.58, ...), custom_call_target="tpu_custom_call" | custom-call | flops 60000002048 | bytes 60000000 | tf_op jit(solution)/shard_map/return_exchange/pallas_call | solution.py:489
  474.1 0.9 reduce_sum.91
  476.2 1.5 fusion.47
  477.7 2.3 fusion.46
  480.0 62.5 %conditional.3 = (bf16[4748,2048]{1,0:T(8,128)(2,1)}) conditional(s32[]{:T(128)} %convert_element_type.95, (s32[32,160]{1,0:T(8,128)S(1)}, bf16[5120,2048]{1,0:T(8,128)(2,1)}) %tuple.119, (s32[]{:T(128)}, s32[32,256]{1,0:T(8,128)}, s32[]{:T(128)}, bf16[256,2048]{1,0:T(8,128)(2,1)S(1)}) %tuple.120), branch_computations={%region_14.18_spmd, %region_17.22_spmd} | conditional | flops 30000037888 | bytes 143479168 | solution.py:795
  482.0 60.5 %table_sum.1 = bf16[4748,2048]{1,0:T(8,128)(2,1)} custom-call(s32[10]{0:T(128)} %get-tuple-element.364.low_ref, s32[10]{0:T(128)} %get-tuple-element.363.high_ref, bf16[32,160,2048]{2,1,0:T(8,128)(2,1)} %bitcast.72, s32[10,1,512]{2,1,0:T(1,128)} %reshape.284.row_ref), custom_call_target="tpu_custom_call" | custom-call | flops 30000001024 | bytes 45000000 | tf_op jit(solution)/shard_map/cond/branch_0_fun/table_sum/pallas_call | solution.py:563
  542.5 1.0 copy.69
  (85 shorter events, 17.8 us)
Async XLA Ops:
  7.2 229.1 %all-gather.2.cloned.1.call-start = ((), (), s32[]{:S(2)}) async-start(), calls=%async_computation | async-start | bytes 19464192 | tf_op jit(solution)/shard_map/all_gather | solution.py:717
  33.5 0.6 copy-start.7
  34.2 198.2 %copy-start.10 = (s32[32,256]{1,0:T(8,128)}, s32[32,256]{1,0:T(8,128)S(1)}, u32[]{:S(2)}) copy-start(s32[32,256]{1,0:T(8,128)S(1)} %slice_convert_fusion) | copy-start | bytes 98308
  34.2 47.9 %copy-start.14 = (s32[1,256]{1,0:T(1,128)S(1)}, s32[1,256]{1,0:T(1,128)}, u32[]{:S(2)}) copy-start(s32[1,256]{1,0:T(1,128)} %param.21) | copy-start | bytes 3076
  234.6 1.4 copy-start
  234.6 2.0 copy-start.3
  236.3 7.1 %copy-start.5 = (bf16[256,2048]{1,0:T(8,128)(2,1)}, bf16[256,2048]{1,0:T(8,128)(2,1)S(1)}, u32[]{:S(2)}) copy-start(bf16[256,2048]{1,0:T(8,128)(2,1)S(1)} %multiply_convert_fusion.hidden) | copy-start | bytes 3145732
  251.7 27.0 %copy-start.1 = (f32[256,2048]{1,0:T(8,128)S(1)}, f32[256,2048]{1,0:T(8,128)}, u32[]{:S(2)}) copy-start(f32[256,2048]{1,0:T(8,128)} %copy-done) | copy-start | bytes 6291460
  278.7 6.4 %copy-start.2 = (f32[256,2048]{1,0:T(8,128)S(1)}, f32[256,2048]{1,0:T(8,128)}, u32[]{:S(2)}) copy-start(f32[256,2048]{1,0:T(8,128)} %copy-done) | copy-start | bytes 6291460
  285.9 4.0 copy-start.11
  285.9 4.6 copy-start.13
  285.9 5.3 copy-start.12
  287.2 7.8 %copy-start.6 = (bf16[256,2048]{1,0:T(8,128)(2,1)S(1)}, bf16[256,2048]{1,0:T(8,128)(2,1)}, u32[]{:S(2)}) copy-start(bf16[256,2048]{1,0:T(8,128)(2,1)} %get-tuple-element.301) | copy-start | bytes 3145732
  287.2 7.8 %copy-start.9 = (bf16[256,256]{1,0:T(8,128)(2,1)S(1)}, bf16[256,256]{1,0:T(8,128)(2,1)}, u32[]{:S(2)}) copy-start(bf16[256,256]{1,0:T(8,128)(2,1)} %get-tuple-element.302) | copy-start | bytes 393220
  474.0 5.9 %copy-start.8 = (s32[32,160]{1,0:T(8,128)S(1)}, s32[32,160]{1,0:T(8,128)}, u32[]{:S(2)}) copy-start(s32[32,160]{1,0:T(8,128)} %copy-done.7) | copy-start | bytes 61444
  480.0 62.5 %copy-start.4 = (bf16[256,2048]{1,0:T(8,128)(2,1)S(1)}, bf16[256,2048]{1,0:T(8,128)(2,1)}, u32[]{:S(2)}) copy-start(bf16[256,2048]{1,0:T(8,128)(2,1)} %get-tuple-element.309) | copy-start | bytes 3145732
Sparse Core Ops, SparseCore 0:
  11.5 167.9 all-gather.1

commit v3 on v2

--- a/solution.py
+++ b/solution.py
@@ -19,13 +19,14 @@
 MESH = pl.DeviceIdType.MESH
 
 
-RELAYS = {2: (26, 18, 10, 6), 3: (27, 19, 11), 4: (28, 20, 12), 5: (29, 21, 13, 7), 8: (30, 22, 14), 9: (31, 23, 15)}
+LOOKUP_RELAYS = {2: (26, 18, 10, 6), 3: (27, 19, 11, 7), 4: (28, 20, 12, 14), 5: (29, 21, 13, 15), 8: (30, 22), 9: (31, 23)}
+RETURN_RELAYS = {2: (26, 18, 10, 6), 3: (27, 19, 11), 4: (28, 20, 12), 5: (29, 21, 13, 7), 8: (30, 22, 14), 9: (31, 23, 15)}
 N_RELAY = 4
 RELAY_STEPS = (6, 9, 12, 15)
 
 
-def far_blocks():
-    return [(ends[k], via, k) for k in range(N_RELAY) for via, ends in RELAYS.items() if k < len(ends)]
+def far_blocks(relays):
+    return [(ends[k], via, k) for k in range(N_RELAY) for via, ends in relays.items() if k < len(ends)]
 
 
 def near_blocks():
@@ -83,8 +84,8 @@
     return ref.at[pl.ds(pl.multiple_of(start, 16), rows)]
 
 
-def on_relays(me, body):
-    for via, ends in RELAYS.items():
+def on_relays(me, relays, body):
+    for via, ends in relays.items():
         @pl.when(me == via)
         def _(ends=ends):
             body(ends)
@@ -124,7 +125,7 @@
 
     @pl.when(me == 0)
     def _():
-        far, near = far_blocks(), near_blocks()
+        far, near = far_blocks(LOOKUP_RELAYS), near_blocks()
         for dev, via, k in far[:6]:
             far_copy(dev, via, k).start()
         for dev in near[:4]:
@@ -156,7 +157,7 @@
         for k in range(len(ends)):
             onward(k).wait_send()
 
-    on_relays(me, pass_on)
+    on_relays(me, LOOKUP_RELAYS, pass_on)
 
     def arrived(off, carry):
         src, copy = cold_from(off)
@@ -172,7 +173,7 @@
     @pl.when(me == 0)
     def _():
         own_hot.wait()
-        for dev, via, k in far_blocks():
+        for dev, via, k in far_blocks(LOOKUP_RELAYS):
             far_copy(dev, via, k).wait_send()
         for dev in near_blocks():
             near_copy(dev).wait_send()
@@ -263,7 +264,7 @@
         def _(dev=dev):
             near_copy(dev).start()
 
-    for dev, via, k in far_blocks():
+    for dev, via, k in far_blocks(RETURN_RELAYS):
         @pl.when(me == dev)
         def _(via=via, k=k):
             far_copy(via, k).start()
@@ -430,7 +431,7 @@
                     pltpu.make_async_copy(relay.at[k], relay.at[k], rr_sem.at[k]).wait()
                     onward(ends, k).start()
 
-        on_relays(me, pass_on)
+        on_relays(me, RETURN_RELAYS, pass_on)
         return carry
 
     lax.fori_loop(0, groups + 2 + 3 * LAG, run, 0)
@@ -439,7 +440,7 @@
         for k in range(len(ends)):
             onward(ends, k).wait_send()
 
-    on_relays(me, passed)
+    on_relays(me, RETURN_RELAYS, passed)
 
     for buf, sem in ((got0, s0_sem), (send1, s1_sem), (send2, s2_sem), (send3, s3_sem)):
         pltpu.make_async_copy(buf, buf, sem).wait()
@@ -603,28 +604,22 @@
 
     q_lin = q_ref[...]
     q_rot = (q_lin * cos_t + turn(q_lin) * sin_t).astype(jnp.bfloat16)
-    seq = q_lin.shape[0]
-    part = seq // 2
-    d_qrot = []
-    for low in (0, part):
-        seen = low + part
-        at, keys = slice(low, seen), slice(0, seen)
-        scores = lax.dot_general(q_rot[at], k_rot[keys], rows_t, preferred_element_type=f32) * scale
-        causal = low + lax.broadcasted_iota(jnp.int32, (part, seen), 0) >= lax.broadcasted_iota(jnp.int32, (part, seen), 1)
-        scores = jnp.where(causal, scores, MASK_VALUE)
-        weight = jnp.exp(scores - jnp.max(scores, axis=1, keepdims=True))
-        prob_f = weight * (1.0 / jnp.sum(weight, axis=1, keepdims=True))
-        prob_b = prob_f.astype(jnp.bfloat16)
-        attn_ref[at] = jnp.dot(prob_b, v_val[keys], preferred_element_type=f32).astype(jnp.bfloat16)
-
-        d_attn = d_attn_ref[at]
-        d_probs = lax.dot_general(d_attn, v_val[keys], rows_t, preferred_element_type=f32)
-        dv_sum[keys] += lax.dot_general(prob_b, d_attn, cols_t, preferred_element_type=f32)
-        d_scores = prob_f * (d_probs - jnp.sum(d_probs * prob_f, axis=1, keepdims=True))
-        d_scores = (d_scores * scale).astype(jnp.bfloat16)
-        d_qrot.append(jnp.dot(d_scores, k_rot[keys], preferred_element_type=f32))
-        dk_sum[keys] += lax.dot_general(d_scores, q_rot[at], cols_t, preferred_element_type=f32)
-    d_qrot = jnp.concatenate(d_qrot, axis=0)
+    scores = lax.dot_general(q_rot, k_rot[...], rows_t, preferred_element_type=f32) * scale
+    seq = scores.shape[0]
+    causal = lax.broadcasted_iota(jnp.int32, (seq, seq), 0) >= lax.broadcasted_iota(jnp.int32, (seq, seq), 1)
+    scores = jnp.where(causal, scores, MASK_VALUE)
+    weight = jnp.exp(scores - jnp.max(scores, axis=1, keepdims=True))
+    prob_f = weight * (1.0 / jnp.sum(weight, axis=1, keepdims=True))
+    prob_b = prob_f.astype(jnp.bfloat16)
+    attn_ref[...] = jnp.dot(prob_b, v_val[...], preferred_element_type=f32).astype(jnp.bfloat16)
+
+    d_attn = d_attn_ref[...]
+    d_probs = lax.dot_general(d_attn, v_val[...], rows_t, preferred_element_type=f32)
+    dv_sum[...] += lax.dot_general(prob_b, d_attn, cols_t, preferred_element_type=f32)
+    d_scores = prob_f * (d_probs - jnp.sum(d_probs * prob_f, axis=1, keepdims=True))
+    d_scores = (d_scores * scale).astype(jnp.bfloat16)
+    d_qrot = jnp.dot(d_scores, k_rot[...], preferred_element_type=f32)
+    dk_sum[...] += lax.dot_general(d_scores, q_rot, cols_t, preferred_element_type=f32)
     d_query = d_qrot * cos_t - turn(d_qrot) * sin_t
     dq_ref[...] = d_query.astype(jnp.bfloat16)
     gq_ref[...] = jnp.sum(d_query, axis=0, keepdims=True)

time: 554 us -> 540 us (0.975); the launches traced: 550 us -> 542 us
  Pallas kernels: 426 us -> 418 us
    pallas_call x1, Pallas kernels: 150 us -> 136 us  [lookup_exchange(): pl.pallas_call(lookup_kernel, out_shape=(jax.ShapeDtypeStruct((HOT_CAP, w...]
    pallas_call x1, Pallas kernels: 176 us -> 185 us  [return_exchange(): pl.pallas_call(return_kernel, out_shape=(jax.ShapeDtypeStruct((N_DEV * HO...]
    pallas_call x1, Pallas kernels: 27 us -> 19.5 us  [attention(): pl.pallas_call(attention_kernel, grid=(heads,), in_specs=[cols(own), cols...]
  transfers between devices with their start and end apart: 1 -> 1, of which waited for: 0 -> 0; matrix products, arithmetic and copies ran while one was open for 11% -> 12% of each run, Pallas kernels for 29% -> 27%
where the time goes in v3:
time: 540 us; the launch traced here: 542 us
  Pallas kernels  418 us (77%)
  local copies, waits for them, and re-layouts  61.7 us (11%)
  matrix products  27.1 us (5%)
  other arithmetic  19.4 us (4%)
  between operations  15.7 us (3%)
    pallas_call x1, Pallas kernels, return_exchange(): pl.pallas_call(return_kernel, out_shape=(jax.ShapeDtypeStruct((N_DEV * HO...  185 us
    pallas_call x1, Pallas kernels, lookup_exchange(): pl.pallas_call(lookup_kernel, out_shape=(jax.ShapeDtypeStruct((HOT_CAP, w...  136 us
    pallas_call x1, Pallas kernels, table_sum(): pl.pallas_call(table_sum_kernel, grid_spec=pltpu.PrefetchScalarGridSpec(n...  65.6 us
    gather x1, local copies, waits for them, and re-layouts, device_step(): jnp.take(table_part, jnp.maximum(rows, 0), axis=0, mode='clip')  47.9 us
    pallas_call x1, Pallas kernels, attention(): pl.pallas_call(attention_kernel, grid=(heads,), in_specs=[cols(own), cols...  19.5 us
    pallas_call x1, Pallas kernels, small_gather(): pl.pallas_call(small_gather_kernel, out_shape=jax.ShapeDtypeStruct((N_DEV...  12.6 us
  transfers between devices with their start and end apart: 1, of which 0 were waited for; matrix products, arithmetic and copies ran while one was open for 12% of the time, Pallas kernels for 27%

profile of v3, /device:TPU:0, one launch (start us, length us, event | category | flops | bytes accessed | tf_op | source)
XLA Modules:
  0.0 542.3 jit_solution(9070321337032230099)
XLA Ops:
  7.2 1.9 pad_maximum_fusion.1
  11.3 12.6 %small_gather.1 = f32[32,8,128]{2,1,0:T(8,128)} custom-call(f32[8,128]{1,0:T(8,128)} %maximum_bitcast_fusion.src), custom_call_target="tpu_custom_call" | custom-call | tf_op jit(solution)/shard_map/small_gather/pallas_call | solution.py:72
  23.9 0.9 copy.43
  24.8 0.9 copy.42
  29.6 2.6 convert_reduce_fusion
  32.2 1.2 select_reduce_fusion
  34.2 47.9 %gather_fusion.1 = bf16[5120,2048]{1,0:T(8,128)(2,1)} fusion(bf16[4748,2048]{1,0:T(8,128)(2,1)} %param.23, s32[5120]{0:T(1024)S(1)} %broadcast_clamp_fusion), kind=kCustom, calls=%fused_computation.1 | custom fusion | bytes 41963520 | tf_op jit(solution)/shard_map/jit(_take)/gather | solution.py:731
  82.6 135.7 %lookup_exchange.1 = (bf16[160,2048]{1,0:T(8,128)(2,1)S(1)}, bf16[496,2048]{1,0:T(8,128)(2,1)S(1)}) custom-call(bf16[5120,2048]{1,0:T(8,128)(2,1)} %gather_fusion.1), custom_call_target="tpu_custom_call" | custom-call | flops 60000002048 | bytes 30000000 | tf_op jit(solution)/shard_map/lookup_exchange/pallas_call | solution.py:196
  218.3 2.2 conditional.2
  218.8 1.8 multiply_reduce_fusion
  222.6 6.7 %fusion.18.d_attn_ref = bf16[256,2048]{1,0:T(8,128)(2,1)} fusion(bf16[2048,4608]{1,0:T(8,128)(2,1)} %all-gather.2.cloned.1.call-done.w_all, bf16[1,256,2048]{2,1,0:T(8,128)(2,1)S(1)} %copy-done.3), kind=kOutput, calls=%fused_computation.43 | convolution fusion | flops 2148007936 | bytes 10485760 | tf_op jit(solution)/shard_map/lo,io->li/dot_general | solution.py:687
  229.3 8.3 %fusion.12.q_ref.k_ref.v_ref = f32[256,2560]{1,0:T(8,128)} fusion(bf16[256,2048]{1,0:T(8,128)(2,1)S(1)} %multiply_convert_fusion.hidden, bf16[2048,4608]{1,0:T(8,128)(2,1)} %all-gather.2.cloned.1.call-done.w_all, f32[2560]{0:T(1024)S(1)} %maximum_convert_fusion), kind=kOutput, calls=%fused_computation.40 | convolution fusion | flops 2685009920 | bytes 14166016 | tf_op jit(solution)/shard_map/dot_general | solution.py:686
  237.7 19.5 %attention.1 = (bf16[256,2048]{1,0:T(8,128)(2,1)}, bf16[256,2048]{1,0:T(8,128)(2,1)}, bf16[256,256]{1,0:T(8,128)(2,1)}, bf16[256,256]{1,0:T(8,128)(2,1)}, f32[1,...) custom-call(f32[256,2560]{1,0:T(8,128)} %fusion.12.q_ref.k_ref.v_ref, f32[256,2560]{1,0:T(8,128)} %fusion.12.q_ref.k_ref.v_ref, ...), custom_call_target="tpu_custom_call" | custom-call | flops 1879048192 | bytes 10000000 | tf_op jit(solution)/shard_map/attention/pallas_call | solution.py:655
  257.2 6.4 %multiply_reduce_fusion.2 = (f32[2048]{0:T(1024)S(1)}, f32[256]{0:T(256)S(1)}, f32[256,2048]{1,0:T(8,128)S(1)}) fusion(f32[256,2048]{1,0:T(8,128)S(1)} %copy-done.1, f32[256]{0:T(256)S(1)} %bitcast.61, f32[2048]{0:T(1024)S(1)} %reshape.248, bf16[2048,4608]{1,0:T(8,128)(2,1)} %all-gather.2.cloned.1.call-done.w_all, bf16[256,256]{1,0:T(8,128)(2,1)} %get-tuple-element.303, ...), kind=kOutput, calls=%fused_computation.46 | convolution fusion | flops 2691430144 | bytes 16009216 | tf_op jit(solution)/shard_map/lo,io->li/dot_general | solution.py:691
  264.4 1.3 convolution_convert_fusion.1.hot_send
  265.7 2.1 convolution_convert_fusion.cold_send
  273.4 2.6 pad_maximum_fusion.grads
  276.0 184.9 %return_exchange.1 = (bf16[5120,2048]{1,0:T(8,128)(2,1)}, f32[32,8,128]{2,1,0:T(8,128)}, f32[64,4608]{1,0:T(8,128)}, bf16[256,2048]{1,0:T(8,128)(2,1)}) custom-call(bf16[160,2048]{1,0:T(8,128)(2,1)} %convolution_convert_fusion.1.hot_send, bf16[496,2048]{1,0:T(8,128)(2,1)} %convolution_convert_fusion.cold_send, f32[32,8,128]{2,1,0:T(8,128)} %bitcast.58, ...), custom_call_target="tpu_custom_call" | custom-call | flops 60000002048 | bytes 60000000 | tf_op jit(solution)/shard_map/return_exchange/pallas_call | solution.py:490
  460.9 0.9 reduce_sum.91
  463.1 1.5 fusion.47
  464.6 2.3 fusion.46
  466.9 67.6 %conditional.3 = (bf16[4748,2048]{1,0:T(8,128)(2,1)}) conditional(s32[]{:T(128)} %convert_element_type.95, (s32[32,160]{1,0:T(8,128)S(1)}, bf16[5120,2048]{1,0:T(8,128)(2,1)}) %tuple.119, (s32[]{:T(128)}, s32[32,256]{1,0:T(8,128)}, s32[]{:T(128)}, bf16[256,2048]{1,0:T(8,128)(2,1)S(1)}) %tuple.120), branch_computations={%region_14.18_spmd, %region_17.22_spmd} | conditional | flops 30000037888 | bytes 143479168 | solution.py:790
  468.9 65.6 %table_sum.1 = bf16[4748,2048]{1,0:T(8,128)(2,1)} custom-call(s32[10]{0:T(128)} %get-tuple-element.364.low_ref, s32[10]{0:T(128)} %get-tuple-element.363.high_ref, bf16[32,160,2048]{2,1,0:T(8,128)(2,1)} %bitcast.72, s32[10,1,512]{2,1,0:T(1,128)} %reshape.284.row_ref), custom_call_target="tpu_custom_call" | custom-call | flops 30000001024 | bytes 45000000 | tf_op jit(solution)/shard_map/cond/branch_0_fun/table_sum/pallas_call | solution.py:564
  534.5 1.0 copy.69
  (85 shorter events, 17.8 us)
Async XLA Ops:
  7.2 215.1 %all-gather.2.cloned.1.call-start = ((), (), s32[]{:S(2)}) async-start(), calls=%async_computation | async-start | bytes 19464192 | tf_op jit(solution)/shard_map/all_gather | solution.py:712
  33.5 0.6 copy-start.7
  34.2 184.1 %copy-start.10 = (s32[32,256]{1,0:T(8,128)}, s32[32,256]{1,0:T(8,128)S(1)}, u32[]{:S(2)}) copy-start(s32[32,256]{1,0:T(8,128)S(1)} %slice_convert_fusion) | copy-start | bytes 98308
  34.2 47.9 %copy-start.14 = (s32[1,256]{1,0:T(1,128)S(1)}, s32[1,256]{1,0:T(1,128)}, u32[]{:S(2)}) copy-start(s32[1,256]{1,0:T(1,128)} %param.21) | copy-start | bytes 3076
  220.5 1.4 copy-start
  220.6 2.0 copy-start.3
  222.2 7.1 %copy-start.5 = (bf16[256,2048]{1,0:T(8,128)(2,1)}, bf16[256,2048]{1,0:T(8,128)(2,1)S(1)}, u32[]{:S(2)}) copy-start(bf16[256,2048]{1,0:T(8,128)(2,1)S(1)} %multiply_convert_fusion.hidden) | copy-start | bytes 3145732
  237.7 19.5 %copy-start.1 = (f32[256,2048]{1,0:T(8,128)S(1)}, f32[256,2048]{1,0:T(8,128)}, u32[]{:S(2)}) copy-start(f32[256,2048]{1,0:T(8,128)} %copy-done) | copy-start | bytes 6291460
  257.2 6.4 %copy-start.2 = (f32[256,2048]{1,0:T(8,128)S(1)}, f32[256,2048]{1,0:T(8,128)}, u32[]{:S(2)}) copy-start(f32[256,2048]{1,0:T(8,128)} %copy-done) | copy-start | bytes 6291460
  264.3 4.0 copy-start.11
  264.3 4.6 copy-start.13
  264.4 5.3 copy-start.12
  265.7 7.8 %copy-start.6 = (bf16[256,2048]{1,0:T(8,128)(2,1)S(1)}, bf16[256,2048]{1,0:T(8,128)(2,1)}, u32[]{:S(2)}) copy-start(bf16[256,2048]{1,0:T(8,128)(2,1)} %get-tuple-element.301) | copy-start | bytes 3145732
  265.7 7.8 %copy-start.9 = (bf16[256,256]{1,0:T(8,128)(2,1)S(1)}, bf16[256,256]{1,0:T(8,128)(2,1)}, u32[]{:S(2)}) copy-start(bf16[256,256]{1,0:T(8,128)(2,1)} %get-tuple-element.302) | copy-start | bytes 393220
  460.9 5.9 %copy-start.8 = (s32[32,160]{1,0:T(8,128)S(1)}, s32[32,160]{1,0:T(8,128)}, u32[]{:S(2)}) copy-start(s32[32,160]{1,0:T(8,128)} %copy-done.7) | copy-start | bytes 61444
  466.9 67.6 %copy-start.4 = (bf16[256,2048]{1,0:T(8,128)(2,1)S(1)}, bf16[256,2048]{1,0:T(8,128)(2,1)}, u32[]{:S(2)}) copy-start(bf16[256,2048]{1,0:T(8,128)(2,1)} %get-tuple-element.309) | copy-start | bytes 3145732
Sparse Core Ops, SparseCore 0:
  11.5 167.9 all-gather.1
